TPU v7x, 32 devices: a 4x4x1 block of a 4x4x8 slice. The times are simulated.
32 devices in a mesh: dp: 1 (over z), tp: 32 (over y, x, core).
Axes of the slice: x: 4, y: 4, z: 1, core: 2. Of those that a mesh axis runs over, the one named last changes fastest.
The devices are a block of a 4x4x8 slice.
Arguments:
- x: bfloat16 [8192, 2048], P(('dp', 'tp'))
- dy: bfloat16 [8192, 2048], P(('dp', 'tp'))
- wg: bfloat16 [2048, 8192], P(None, 'tp')
- wu: bfloat16 [2048, 8192], P(None, 'tp')
- wd: bfloat16 [8192, 2048], P('tp')
- ug: bfloat16 [8192, 8192], P('dp', 'tp')
- uu: bfloat16 [8192, 8192], P('dp', 'tp')
Outputs:
- output 1: bfloat16 [8192, 2048], P(('dp', 'tp'))
- output 2: float32 [2048, 8192], P('dp', 'tp')
- output 3: float32 [2048, 8192], P('dp', 'tp')
- output 4: float32 [8192, 2048], P(('dp', 'tp'))
All inputs are finite; a program needn't handle non-finite values.
Results may differ from a plain program's by a relative error of at most 0.0143732.
Values are sent between devices in bfloat16 or wider.
A program may use at most 768 MiB of HBM per device.

v0:
```python
import jax
import jax.numpy as jnp
from jax import lax
from jax.sharding import PartitionSpec as P


def solution(mesh):
    tok = P(("dp", "tp"), None)
    col = P(None, "tp")
    row = P("tp", None)
    act = P("dp", "tp")

    def body(x, dy, wg, wu, wd, ug, uu):
        xg = lax.all_gather(x, "tp", axis=0, tiled=True)
        dyg = lax.all_gather(dy, "tp", axis=0, tiled=True)
        ug32 = ug.astype(jnp.float32)
        uu32 = uu.astype(jnp.float32)
        s = jax.nn.sigmoid(ug32)
        a = ug32 * s
        z = (a * uu32).astype(jnp.bfloat16)
        dwd = jnp.dot(z.T, dyg, preferred_element_type=jnp.float32)
        g = jnp.dot(dyg, wd.T, preferred_element_type=jnp.float32)
        duu = (g * a).astype(jnp.bfloat16)
        dug = (g * uu32 * s * (1.0 + ug32 * (1.0 - s))).astype(jnp.bfloat16)
        p = jnp.dot(dug, wg.T, preferred_element_type=jnp.float32) + jnp.dot(duu, wu.T, preferred_element_type=jnp.float32)
        dx = lax.psum_scatter(p.astype(jnp.bfloat16), "tp", scatter_dimension=0, tiled=True)
        dwg = jnp.dot(xg.T, dug, preferred_element_type=jnp.float32)
        dwu = jnp.dot(xg.T, duu, preferred_element_type=jnp.float32)
        return dx, dwg, dwu, dwd

    return jax.shard_map(body, mesh=mesh, in_specs=(tok, tok, col, col, row, act, act), out_specs=(tok, act, act, tok), check_vma=False)
```

profile of v0, /device:TPU:97, one launch (start us, length us, event | category | flops | bytes accessed | tf_op | source)
XLA Modules:
  0.0 398.0 jit_solution(16479374450681291817)
XLA Ops:
  7.2 0.0 copy-start
  7.2 0.1 all-gather.3.cloned.1.call-start
  7.3 0.7 all-gather.3.cloned.1.call-update
  8.0 0.1 all-gather.5.cloned.1.call-start
  8.1 0.7 all-gather.5.cloned.1.call-update
  8.8 0.1 reduce-scatter.2.cloned.1.call-start
  8.9 113.8 %all-gather.3.cloned.1.call-done = bf16[8192,2048]{1,0:T(8,128)(2,1)} async-done(((bf16[256,2048]{1,0:T(8,128)(2,1)}), bf16[8192,2048]{1,0:T(8,128)(2,1)}) %all-gather.3.cloned.1.call-update) | async-done | bytes 33554448 | tf_op jit(solution)/shard_map/all_gather | solution.py:15
  122.6 23.3 %fusion.2 = (bf16[8192,256]{1,0:T(8,128)(2,1)}, f32[8192,256]{1,0:T(8,128)}) fusion(bf16[8192,256]{1,0:T(8,128)(2,1)} %param.13, bf16[8192,256]{1,0:T(8,128)(2,1)} %param.12, bf16[8192,2048]{1,0:T(8,128)(2,1)} %all-gather.3.cloned.1.call-done, bf16[256,2048]{1,0:T(8,128)(2,1)} %param.11), kind=kOutput, calls=%fused_computation.8 | convolution fusion | flops 8615100416 | bytes 55574528 | tf_op jit(solution)/shard_map/dot_general | solution.py:22
  145.9 0.0 copy-done
  145.9 0.0 copy-start.2
  145.9 25.4 %fusion.11 = f32[8192,2048]{1,0:T(8,128)} fusion(bf16[8192,256]{1,0:T(8,128)(2,1)} %get-tuple-element.8, bf16[2048,256]{1,0:T(8,128)(2,1)S(1)} %copy-done), kind=kOutput, calls=%fused_computation.19 | convolution fusion | flops 8589934592 | bytes 72351744 | tf_op jit(solution)/shard_map/dot_general | solution.py:25
  171.3 0.0 copy-done.2
  171.3 38.2 %add_convert_fusion = bf16[8192,2048]{1,0:T(8,128)(2,1)} fusion(f32[8192,2048]{1,0:T(8,128)} %fusion.11, bf16[2048,256]{1,0:T(8,128)(2,1)S(1)} %copy-done.2, f32[8192,256]{1,0:T(8,128)} %get-tuple-element.9, bf16[8192,256]{1,0:T(8,128)(2,1)} %param.12), kind=kOutput, calls=%fused_computation | convolution fusion | flops 8638169088 | bytes 114294784 | tf_op jit(solution)/shard_map/dot_general | solution.py:25
  209.6 0.1 reduce-scatter.2.cloned.1.call-update
  209.6 22.6 %all-gather.5.cloned.1.call-done = bf16[8192,2048]{1,0:T(8,128)(2,1)} async-done(((bf16[256,2048]{1,0:T(8,128)(2,1)}), bf16[8192,2048]{1,0:T(8,128)(2,1)}) %all-gather.5.cloned.1.call-update) | async-done | bytes 33554448 | tf_op jit(solution)/shard_map/all_gather | solution.py:14
  232.2 18.9 %convolution_bitcast_fusion = f32[2048,256]{0,1:T(8,128)S(1)} fusion(bf16[8192,2048]{1,0:T(8,128)(2,1)} %all-gather.5.cloned.1.call-done, f32[8192,256]{1,0:T(8,128)} %get-tuple-element.9, bf16[8192,256]{1,0:T(8,128)(2,1)} %param.12), kind=kOutput, calls=%fused_computation.16 | convolution fusion | flops 8604614656 | bytes 48234496 | tf_op jit(solution)/shard_map/dot_general | solution.py:28
  251.1 1.8 copy.12
  252.9 16.3 %convolution_bitcast_fusion.1 = f32[2048,256]{0,1:T(8,128)S(1)} fusion(bf16[8192,256]{1,0:T(8,128)(2,1)} %get-tuple-element.8, bf16[8192,2048]{1,0:T(8,128)(2,1)} %all-gather.5.cloned.1.call-done), kind=kOutput, calls=%fused_computation.17 | convolution fusion | flops 8589934592 | bytes 39845888 | tf_op jit(solution)/shard_map/dot_general | solution.py:27
  269.3 1.8 copy.11
  271.1 0.0 copy-start.1
  271.1 19.0 %fusion.8 = f32[256,2048]{1,0:T(8,128)} fusion(bf16[8192,2048]{1,0:T(8,128)(2,1)} %all-gather.3.cloned.1.call-done, bf16[8192,256]{1,0:T(8,128)(2,1)} %param.13, bf16[8192,256]{1,0:T(8,128)(2,1)} %param.12), kind=kOutput, calls=%fused_computation.15 | convolution fusion | flops 8606711808 | bytes 44040192 | tf_op jit(solution)/shard_map/dot_general | solution.py:21
  290.1 101.4 %reduce-scatter.2.cloned.1.call-done = bf16[256,2048]{1,0:T(8,128)(2,1)} async-done(((bf16[8192,2048]{1,0:T(8,128)(2,1)}), bf16[256,2048]{1,0:T(8,128)(2,1)}) %reduce-scatter.2.cloned.1.call-update) | async-done | bytes 1048592 | tf_op jit(solution)/shard_map/reduce_scatter | solution.py:26
  391.5 0.0 copy-done.1
Async XLA Ops:
  7.2 138.8 %copy-start = (bf16[2048,256]{1,0:T(8,128)(2,1)S(1)}, bf16[2048,256]{1,0:T(8,128)(2,1)}, u32[]{:S(2)}) copy-start(bf16[2048,256]{1,0:T(8,128)(2,1)} %param.9) | copy-start | bytes 3145732
  7.2 115.4 %all-gather.3.cloned.1.call-start = ((), (), s32[]{:S(2)}) async-start(), calls=%async_computation.1 | async-start | bytes 34603008 | tf_op jit(solution)/shard_map/all_gather | solution.py:15
  8.0 224.2 %all-gather.5.cloned.1.call-start = ((), (), s32[]{:S(2)}) async-start(), calls=%async_computation.3 | async-start | bytes 34603008 | tf_op jit(solution)/shard_map/all_gather | solution.py:14
  8.8 382.7 %reduce-scatter.2.cloned.1.call-start = ((), (), s32[]{:S(2)}) async-start(), calls=%async_computation.2 | async-start | bytes 34603008 | tf_op jit(solution)/shard_map/reduce_scatter | solution.py:26
  145.9 25.4 %copy-start.2 = (bf16[2048,256]{1,0:T(8,128)(2,1)S(1)}, bf16[2048,256]{1,0:T(8,128)(2,1)}, u32[]{:S(2)}) copy-start(bf16[2048,256]{1,0:T(8,128)(2,1)} %param.10) | copy-start | bytes 3145732
  271.1 120.4 %copy-start.1 = (bf16[2048,256]{1,0:T(8,128)(2,1)S(1)}, bf16[2048,256]{1,0:T(8,128)(2,1)}, u32[]{:S(2)}) copy-start(bf16[2048,256]{1,0:T(8,128)(2,1)} %param.9) | copy-start | bytes 3145732
Sparse Core Ops, SparseCore 0:
  10.1 112.4 all-gather.2
  124.7 107.4 all-gather.4
  236.5 154.9 reduce-scatter.1
where the time goes:
time: 398 us
  waiting for transfers between devices  239 us (60%)
  matrix products  141 us (35%)
  between operations  13.8 us (3%)
    all_gather x1, waiting for transfers between devices, body(): dyg = lax.all_gather(dy, 'tp', axis=0, tiled=True)  114 us
    reduce_scatter x1, waiting for transfers between devices, body(): lax.psum_scatter(p.astype(jnp.bfloat16), 'tp', scatter_dimension=0, tiled...  101 us
    dot_general x1, matrix products, body(): jnp.dot(duu, wu.T, preferred_element_type=jnp.float32)  38.2 us
    dot_general x1, matrix products, body(): jnp.dot(dug, wg.T, preferred_element_type=jnp.float32)  25.4 us
    dot_general x1, matrix products, body(): g = jnp.dot(dyg, wd.T, preferred_element_type=jnp.float32)  23.3 us
    all_gather x1, waiting for transfers between devices, body(): xg = lax.all_gather(x, 'tp', axis=0, tiled=True)  22.6 us
    dot_general x1, matrix products, body(): dwd = jnp.dot(z.T, dyg, preferred_element_type=jnp.float32)  19 us
    dot_general x1, matrix products, body(): dwu = jnp.dot(xg.T, duu, preferred_element_type=jnp.float32)  18.9 us
  transfers between devices with their start and end apart: 3, of which 3 were waited for; matrix products, arithmetic and copies ran while one was open for 36% of the time, Pallas kernels for 0%

commit v1 on v0

v1 whole, which is shorter than its diff:
```python
import functools
import math

import jax
import jax.numpy as jnp
from jax import lax
from jax.experimental import pallas as pl
from jax.experimental.pallas import tpu as pltpu
from jax.sharding import PartitionSpec as P

F32 = jnp.float32
BF16 = jnp.bfloat16
S = 4
NR = 4
MESH = pl.DeviceIdType.MESH


def dot(a, b, ca, cb):
    return lax.dot_general(a, b, (((ca,), (cb,)), ((), ())), preferred_element_type=F32)


def kernel(
    n, side,
    x_h, dy_h, wg_h, wu_h, wd_h, ug_h, uu_h,
    dx_h, dwg_h, dwu_h, dwd_h,
    dyb, xb, rsb, rso, pbuf, wdb, wgu, ub, gbuf, dub, zb, accd, accw, recd, recw,
    dy_ss, dy_rs, x_ss, x_rs, rs_ss, rs_rs, u_ss, u_rs, u_ls, w_ss, w_rs, w_ls, own_ls,
    e_ss, e_rs, o_ls,
):
    tb, h = x_h.shape
    fb = wg_h.shape[1]
    rr = tb // NR
    me = lax.axis_index("tp")
    chip = me // 2
    core = lax.rem(me, 2)
    p = chip // side
    q = lax.rem(chip, side)
    pos1 = side * p + lax.rem(q + p, side)
    pos2 = side * q + lax.rem(p + q, side)

    def chip_at(cycle, i):
        a = i // side
        b = lax.rem(lax.rem(i, side) + side - a, side)
        return a * side + b if cycle == 0 else b * side + a

    def ring_chip(r, back):
        here = pos1 if r < 2 else pos2
        d = back if r % 2 == 0 else -back
        return chip_at(r // 2, lax.rem(here - d + 2 * n, n))

    down = [ring_chip(r, -1) * 2 + core for r in range(NR)]
    sib = chip * 2 + 1 - core

    def remote(src, dst, ss, rs, dev):
        return pltpu.make_async_remote_copy(
            src_ref=src, dst_ref=dst, send_sem=ss, recv_sem=rs, device_id={"tp": dev}, device_id_type=MESH
        )

    def hop(buf, ss, rs, s, r):
        a, b = lax.rem(s, S), lax.rem(s + 1, S)
        return remote(buf.at[a, r], buf.at[b, r], ss.at[a, r], rs.at[b, r], down[r])

    def dy_hop(s, r):
        return hop(dyb, dy_ss, dy_rs, s, r)

    def x_hop(s, r):
        return hop(xb, x_ss, x_rs, s, r)

    def rs_hop(s, r):
        a, b = lax.rem(s, 2), lax.rem(s + 1, S)
        return remote(rso.at[a, r], rsb.at[b, r], rs_ss.at[a, r], rs_rs.at[b, r], down[r])

    def u_start(s):
        for r in range(NR):
            o = ring_chip(r, s)
            mine = pl.multiple_of((2 * o + core) * tb + r * rr, rr)
            theirs = pl.multiple_of((2 * o + 1 - core) * tb + r * rr, rr)
            for j, u in enumerate((ug_h, uu_h)):
                pltpu.make_async_copy(u.at[pl.ds(mine, rr)], ub.at[s, 0, j, r], u_ls.at[s]).start()
                remote(u.at[pl.ds(theirs, rr)], ub.at[s, 1, j, r], u_ss.at[s], u_rs.at[s], sib).start()

    weights = ((wd_h, (wdb.at[pl.ds(0, fb)], wdb.at[pl.ds(fb, fb)])),
               (wg_h, (wgu.at[:, pl.ds(0, fb)], wgu.at[:, pl.ds(fb, fb)])),
               (wu_h, (wgu.at[:, pl.ds(2 * fb, fb)], wgu.at[:, pl.ds(3 * fb, fb)])))

    def w_local(i):
        return pltpu.make_async_copy(weights[i][0], weights[i][1][0], w_ls.at[i])

    def w_remote(i):
        return remote(weights[i][0], weights[i][1][1], w_ss.at[i], w_rs.at[i], sib)

    def own(i, r):
        src, dst = ((dy_h, dyb), (x_h, xb))[i]
        return pltpu.make_async_copy(src.at[pl.ds(r * rr, rr)], dst.at[0, r], own_ls.at[i, r])

    barrier = pltpu.get_barrier_semaphore()
    for dev in down + [sib]:
        pl.semaphore_signal(barrier, inc=1, device_id={"tp": dev}, device_id_type=MESH)
    for i in range(2):
        for r in range(NR):
            own(i, r).start()
    for i in range(3):
        w_local(i).start()
    pl.semaphore_wait(barrier, NR + 1)
    for r in range(NR):
        own(0, r).wait()
        dy_hop(0, r).start()
    for i in range(3):
        w_remote(i).start()
    for r in range(NR):
        own(1, r).wait()
        x_hop(0, r).start()
    u_start(0)
    u_start(1)

    def zero(i, _):
        accd[pl.ds(pl.multiple_of(i * (2 * fb // 8), 2 * fb // 8), 2 * fb // 8), :] = jnp.zeros((2 * fb // 8, h), F32)
        accw[pl.ds(pl.multiple_of(i * (h // 8), h // 8), h // 8), :] = jnp.zeros((h // 8, 4 * fb), F32)
        return 0

    lax.fori_loop(0, 8, zero, 0)
    for r in range(NR):
        rsb[1, r] = jnp.zeros((rr, h), BF16)

    ct = min(512, h)
    ht = min(256, h)

    def step(s, _):
        slot = lax.rem(s, S)

        @pl.when(s >= 1)
        def _():
            for r in range(NR):
                dy_hop(s - 1, r).wait_recv()

        @pl.when((s >= 2) & (s < n - 1))
        def _():
            for r in range(NR):
                dy_hop(s - 2, r).wait_send()

        @pl.when((s >= 1) & (s < n - 1))
        def _():
            for r in range(NR):
                dy_hop(s, r).start()

        @pl.when(s + 2 < n)
        def _():
            u_start(s + 2)

        pltpu.make_async_copy(ub.at[s, 0], ub.at[s, 0], u_ls.at[s]).wait()
        u_all = remote(ub.at[s, 1], ub.at[s, 1], u_ss.at[s], u_rs.at[s], sib)
        u_all.wait_recv()

        @pl.when(s == 0)
        def _():
            for i in range(3):
                w_local(i).wait()
                w_remote(i).wait_recv()

        for f in range(2):
            g = dot(dyb[slot].reshape(tb, h), wdb[f * fb:(f + 1) * fb, :], 1, 1)
            gbuf[:, f * fb:(f + 1) * fb] = g
        for f in range(2):
            def act(r, _, f=f):
                rows = pl.ds(pl.multiple_of(r * rr, rr), rr)
                g = gbuf[rows, f * fb:(f + 1) * fb]
                ug = ub[s, f, 0, r].astype(F32)
                uu = ub[s, f, 1, r].astype(F32)
                sg = jax.nn.sigmoid(ug)
                a = ug * sg
                zb[rows, f * fb:(f + 1) * fb] = (a * uu).astype(BF16)
                dub[rows, f * fb:(f + 1) * fb] = (g * uu * sg * (1.0 + ug * (1.0 - sg))).astype(BF16)
                dub[rows, (2 + f) * fb:(3 + f) * fb] = (g * a).astype(BF16)
                return 0

            lax.fori_loop(0, NR, act, 0)

        pi = jnp.where(s == 0, 1, 0)

        def dx_tile(j, _):
            cols = pl.ds(pl.multiple_of(j * ct, ct), ct)
            pbuf[pi, :, cols] = dot(dub[...], wgu[cols, :], 1, 1)
            return 0

        lax.fori_loop(0, h // ct, dx_tile, 0)

        @pl.when(s >= 1)
        def _():
            for r in range(NR):
                x_hop(s - 1, r).wait_recv()

        @pl.when((s >= 2) & (s < n - 1))
        def _():
            for r in range(NR):
                x_hop(s - 2, r).wait_send()

        @pl.when((s >= 1) & (s < n - 1))
        def _():
            for r in range(NR):
                x_hop(s, r).start()

        def dwd_tile(j, _):
            cols = pl.ds(pl.multiple_of(j * ct, ct), ct)
            accd[:, cols] += dot(zb[...], dyb[slot, :, :, cols].reshape(tb, ct), 0, 0)
            return 0

        lax.fori_loop(0, h // ct, dwd_tile, 0)

        @pl.when(s >= 2)
        def _():
            for r in range(NR):
                rs_hop(s - 1, r).wait_recv()

        @pl.when(s >= 3)
        def _():
            for r in range(NR):
                rs_hop(s - 2, r).wait_send()

        @pl.when(s >= 1)
        def _():
            def add(r, _):
                part = pbuf[0, pl.ds(pl.multiple_of(r * rr, rr), rr), :]
                rso[lax.rem(s, 2), r] = (part + rsb[slot, r].astype(F32)).astype(BF16)
                return 0

            lax.fori_loop(0, NR, add, 0)
            for r in range(NR):
                rs_hop(s, r).start()

        def dw_tile(j, _):
            rows = pl.ds(pl.multiple_of(j * ht, ht), ht)
            accw[rows, :] += dot(xb[slot, :, :, rows].reshape(tb, ht), dub[...], 0, 0)
            return 0

        lax.fori_loop(0, h // ht, dw_tile, 0)
        u_all.wait_send()
        return 0

    lax.fori_loop(0, n, step, 0)

    swaps = (remote(accd.at[pl.ds(fb, fb)], recd, e_ss.at[0], e_rs.at[0], sib),
             remote(accw.at[:, pl.ds(fb, fb)], recw.at[0], e_ss.at[1], e_rs.at[1], sib),
             remote(accw.at[:, pl.ds(3 * fb, fb)], recw.at[1], e_ss.at[2], e_rs.at[2], sib))
    for c in swaps:
        c.start()
    for r in range(NR):
        rs_hop(n - 2, r).wait_send()
    outs = []

    swaps[0].wait_recv()
    accd[0:fb, :] += recd[...]
    outs.append(pltpu.make_async_copy(accd.at[pl.ds(0, fb)], dwd_h, o_ls.at[0]))
    outs[-1].start()
    for i, o in enumerate((dwg_h, dwu_h)):
        swaps[1 + i].wait_recv()

        def fold(j, _, i=i):
            rows = pl.ds(pl.multiple_of(j * ht, ht), ht)
            accw[rows, 2 * i * fb:(2 * i + 1) * fb] += recw[i, rows, :]
            return 0

        lax.fori_loop(0, h // ht, fold, 0)
        outs.append(pltpu.make_async_copy(accw.at[:, pl.ds(2 * i * fb, fb)], o, o_ls.at[1 + i]))
        outs[-1].start()

    for r in range(NR):
        rs_hop(n - 1, r).wait_recv()
        rso[0, r] = (pbuf[1, r * rr:(r + 1) * rr, :] + rsb[n % S, r].astype(F32)).astype(BF16)
        outs.append(pltpu.make_async_copy(rso.at[0, r], dx_h.at[pl.ds(r * rr, rr)], o_ls.at[3 + r]))
        outs[-1].start()

    for c in outs:
        c.wait()
    for c in swaps:
        c.wait_send()
    for i in range(3):
        w_remote(i).wait_send()
    for r in range(NR):
        for s in (n - 3, n - 2):
            dy_hop(s, r).wait_send()
            x_hop(s, r).wait_send()
        rs_hop(n - 1, r).wait_send()


def solution(mesh):
    tok = P(("dp", "tp"), None)
    col = P(None, "tp")
    row = P("tp", None)
    act = P("dp", "tp")
    n = mesh.shape["tp"] // 2
    side = math.isqrt(n)

    def body(x, dy, wg, wu, wd, ug, uu):
        tb, h = x.shape
        fb = wg.shape[1]
        rr = tb // NR
        vm = pltpu.VMEM
        dma = pltpu.SemaphoreType.DMA
        flops = 12 * n * tb * h * 2 * fb
        return pl.pallas_call(
            functools.partial(kernel, n, side),
            out_shape=(
                jax.ShapeDtypeStruct((tb, h), BF16),
                jax.ShapeDtypeStruct((h, fb), F32),
                jax.ShapeDtypeStruct((h, fb), F32),
                jax.ShapeDtypeStruct((fb, h), F32),
            ),
            in_specs=[pl.BlockSpec(memory_space=pl.ANY)] * 7,
            out_specs=[pl.BlockSpec(memory_space=pl.ANY)] * 4,
            scratch_shapes=[
                vm((S, NR, rr, h), BF16),
                vm((S, NR, rr, h), BF16),
                vm((S, NR, rr, h), BF16),
                vm((2, NR, rr, h), BF16),
                vm((2, tb, h), F32),
                vm((2 * fb, h), BF16),
                vm((h, 4 * fb), BF16),
                vm((n, 2, 2, NR, rr, fb), BF16),
                vm((tb, 2 * fb), F32),
                vm((tb, 4 * fb), BF16),
                vm((tb, 2 * fb), BF16),
                vm((2 * fb, h), F32),
                vm((h, 4 * fb), F32),
                vm((fb, h), F32),
                vm((2, h, fb), F32),
                dma((S, NR)), dma((S, NR)), dma((S, NR)), dma((S, NR)), dma((2, NR)), dma((S, NR)),
                dma((n,)), dma((n,)), dma((n,)), dma((3,)), dma((3,)), dma((3,)), dma((2, NR)),
                dma((3,)), dma((3,)), dma((3 + NR,)),
            ],
            compiler_params=pltpu.CompilerParams(
                collective_id=0, has_side_effects=True, vmem_limit_bytes=62 * 1024 * 1024
            ),
            cost_estimate=pl.CostEstimate(flops=flops, bytes_accessed=2 * flops // 1000, transcendentals=0),
        )(x, dy, wg, wu, wd, ug, uu)

    return jax.shard_map(
        body, mesh=mesh, in_specs=(tok, tok, col, col, row, act, act), out_specs=(tok, act, act, tok), check_vma=False
    )
```

time: 398 us -> 284 us (0.71)
  Pallas kernels: 0 us -> 275 us
  waiting for transfers between devices: 239 us -> 0 us
  matrix products: 141 us -> 0 us
  between operations: 13.8 us -> 0.65 us
  local copies, waits for them, and re-layouts: 3.65 us -> 8.47 us
    pallas_call x0 -> x1, Pallas kernels: none -> 275 us  [body(): pl.pallas_call(functools.partial(kernel, n, side), out_shape=(jax.ShapeDt...]
    dot_general x6 -> x0, matrix products: 141 us -> none  [the longest x1 38.2 us: body(): jnp.dot(duu, wu.T, preferred_element_type=jnp.float32)]
    all_gather x2 -> x0, waiting for transfers between devices: 136 us -> none  [the longest x1 114 us: body(): dyg = lax.all_gather(dy, 'tp', axis=0, tiled=True)]
    reduce_scatter x1 -> x0, waiting for transfers between devices: 101 us -> none  [body(): lax.psum_scatter(p.astype(jnp.bfloat16), 'tp', scatter_dimension=0, tiled...]
    unnamed x8 -> x10, local copies, waits for them, and re-layouts: 3.65 us -> 8.47 us
  transfers between devices with their start and end apart: 3 -> 0, of which waited for: 3 -> 0; matrix products, arithmetic and copies ran while one was open for 36% -> 0% of each run, Pallas kernels for 0% -> 0%
where the time goes in v1:
time: 284 us
  Pallas kernels  275 us (97%)
  local copies, waits for them, and re-layouts  8.47 us (3%)
    pallas_call x1, Pallas kernels, body(): pl.pallas_call(functools.partial(kernel, n, side), out_shape=(jax.ShapeDt...  275 us
    unnamed x10, local copies, waits for them, and re-layouts  8.47 us

profile of v1, /device:TPU:97, one launch (start us, length us, event | category | flops | bytes accessed | tf_op | source)
XLA Modules:
  0.0 284.0 jit_solution(6287477607696327260)
XLA Ops:
  0.6 274.9 %shard_map.102 = (bf16[256,2048]{1,0:T(8,128)(2,1)}, f32[2048,256]{1,0:T(8,128)}, f32[2048,256]{1,0:T(8,128)}, f32[256,2048]{1,0:T(8,128)}) custom-call(bf16[256,2048]{1,0:T(8,128)(2,1)} %x_h.1, bf16[256,2048]{1,0:T(8,128)(2,1)} %dy_h.1, bf16[2048,256]{1,0:T(8,128)(2,1)} %wg_h.1, bf16[2048,256]{1,0:T(8,128)(2,1)} %wu_h.1, bf16[256,2048]{1,0:T(8,128)(2,1)} %wd_h.1, ...), custom_call_target="tpu_custom_call" | custom-call | flops 51539607552 | bytes 103079216 | tf_op jit(solution)/shard_map/pallas_call | solution.py:300
  275.5 0.0 copy-start.2
  275.5 2.5 copy.15
  278.0 0.0 copy-done.2
  278.0 0.0 copy-start.1
  278.0 1.3 copy.16
  279.3 1.0 copy-done.1
  280.4 0.0 copy-start
  280.4 1.3 copy.17
  281.7 1.0 copy-done
  282.7 1.3 copy.18
Async XLA Ops:
  275.5 2.5 copy-start.2
  278.0 2.3 copy-start.1
  280.4 2.3 copy-start

commit v2 on v0

v2 whole, which is shorter than its diff:
```python
import functools
import math

import jax
import jax.numpy as jnp
from jax import lax
from jax.experimental import pallas as pl
from jax.experimental.pallas import tpu as pltpu
from jax.sharding import PartitionSpec as P

F32 = jnp.float32
BF16 = jnp.bfloat16
S = 4
MESH = pl.DeviceIdType.MESH


def dot(a, b, ca, cb):
    return lax.dot_general(a, b, (((ca,), (cb,)), ((), ())), preferred_element_type=F32)


def kernel(
    side,
    x_h, dy_h, wg_h, wu_h, wd_h, ug_h, uu_h,
    dx_h, own_d, own_g, own_u, rec_d, rec_g, rec_u, dyl, xl,
    dyt, xt, uo, ux, wdb, wgu, gbuf, zb, dub, accd, accw, pbuf, sin, sout, rsb, rso,
    dyr_s, dyr_r, dyc_s, dyc_r, xr_s, xr_r, xc_s, xc_r, dyt_l, xt_l, u_s, u_r, u_l,
    w_s, w_r, w_l, p_s, p_r, rs_s, rs_r, e_s, e_r, o_l,
):
    _, hb, h = dy_h.shape
    tb = 2 * hb
    q4 = hb // 2
    fb = wg_h.shape[1]
    fh = fb // 2
    m = 2 * side
    me = lax.axis_index("tp")
    chip = me // 2
    core = lax.rem(me, 2)
    other = 1 - core
    py = chip // side
    px = lax.rem(chip, side)
    cls = lax.rem(px + py, side)
    grp = cls // 2
    odd = lax.rem(cls, 2)

    def ring_pos(y, odd_):
        return 2 * lax.rem(side - y, side) + odd_

    def chip_at(g, i):
        k = i // 2
        return lax.rem(side - k, side) * side + lax.rem(k + lax.rem(i, 2) + 2 * g, side)

    def origin(g, pos, d, t):
        return chip_at(g, lax.rem(pos + (2 * m - t if d == 0 else t), m))

    pos = ring_pos(py, odd)
    down = [chip_at(grp, lax.rem(pos + 1, m)) * 2 + core, chip_at(grp, lax.rem(pos + m - 1, m)) * 2 + core]
    sib = chip * 2 + other
    step_ = side - 1 + 2 * odd
    mates = []
    for y, x in ((py, lax.rem(px + step_, side)), (lax.rem(py + step_, side), px)):
        c = lax.rem(x + y, side)
        mates.append(((y * side + x) * 2 + core, c // 2, ring_pos(y, lax.rem(c, 2))))

    def remote(src, dst, ss, rs, dev):
        return pltpu.make_async_remote_copy(
            src_ref=src, dst_ref=dst, send_sem=ss, recv_sem=rs, device_id={"tp": dev}, device_id_type=MESH
        )

    rows = ((dy_h, dyl, dyr_s, dyr_r, dyc_s, dyc_r, dyt, dyt_l), (x_h, xl, xr_s, xr_r, xc_s, xc_r, xt, xt_l))

    def ring(i, s, d, first=False):
        src, land, ss, rs = rows[i][:4]
        return remote(src.at[d] if first else land.at[s, core, d], land.at[s + 1, core, d], ss.at[s, d], rs.at[s + 1, d], down[d])

    def cross(i, s, d, first=False):
        src, land, ss, rs = rows[i][0], rows[i][1], rows[i][4], rows[i][5]
        return remote(src.at[d] if first else land.at[s, core, d], land.at[s, core, d], ss.at[s, d], rs.at[s, d], sib)

    def cross_in(i, s, d):
        land, ss, rs = rows[i][1], rows[i][4], rows[i][5]
        return remote(land.at[s, other, d], land.at[s, other, d], ss.at[s, d], rs.at[s, d], sib)

    def tile_wait(i, t):
        tile, sem = rows[i][6], rows[i][7]
        b = lax.rem(t, 2)
        pltpu.make_async_copy(tile.at[b], tile.at[b], sem.at[b]).wait()

    def tile_load(i, t):
        src, land, tile, sem = rows[i][0], rows[i][1], rows[i][6], rows[i][7]
        b = lax.rem(t, 2)
        for d in range(2):
            cross_in(i, t, d).wait_recv()

        @pl.when(t == 0)
        def _():
            pltpu.make_async_copy(src, tile.at[b, core], sem.at[b]).start()
            pltpu.make_async_copy(land.at[t, other], tile.at[b, other], sem.at[b]).start()

        @pl.when(t > 0)
        def _():
            pltpu.make_async_copy(land.at[t], tile.at[b], sem.at[b]).start()

        if i == 0:
            for d in range(2):
                o = origin(grp, pos, d, t)
                for j, u in enumerate((ug_h, uu_h)):
                    pltpu.make_async_copy(u.at[o, :, d], uo.at[b, j, :, d], u_l.at[b]).start()

    def u_send(t, _):
        for k, (dev, g, p) in enumerate(mates):
            for d in range(2):
                o = origin(g, p, d, t)
                for j, u in enumerate((ug_h, uu_h)):
                    remote(u.at[o, :, d, :, pl.ds(k * fh, fh)], ux.at[t, k, j, :, d], u_s.at[t, k], u_r.at[t, k], dev).start()
        return 0

    def u_all(t, k):
        return remote(ux.at[t, k], ux.at[t, k], u_s.at[t, k], u_r.at[t, k], mates[k][0])

    def w_local(i):
        if i == 0:
            return pltpu.make_async_copy(wd_h, wdb.at[pl.ds(0, fb)], w_l.at[i])
        return pltpu.make_async_copy((wg_h, wu_h)[i - 1], wgu.at[:, pl.ds((i - 1) * 2 * fb, fb)], w_l.at[i])

    def w_remote(i, k):
        if i == 0:
            src, dst = wd_h.at[pl.ds(k * fh, fh)], wdb.at[pl.ds(fb + k * fh, fh)]
        else:
            src = (wg_h, wu_h)[i - 1].at[:, pl.ds(k * fh, fh)]
            dst = wgu.at[:, pl.ds((i - 1) * 2 * fb + fb + k * fh, fh)]
        return remote(src, dst, w_s.at[i, k], w_r.at[i, k], mates[k][0])

    def swap(i, k):
        if i == 0:
            src, dst = accd.at[pl.ds(fb + k * fh, fh)], rec_d.at[pl.ds(k * fh, fh)]
        else:
            src = accw.at[:, pl.ds((i - 1) * 2 * fb + fb + k * fh, fh)]
            dst = (rec_g, rec_u)[i - 1].at[:, pl.ds(k * fh, fh)]
        return remote(src, dst, e_s.at[i, k], e_r.at[i, k], mates[k][0])

    def own_out(i):
        if i == 0:
            return pltpu.make_async_copy(accd.at[pl.ds(0, fb)], own_d, o_l.at[0])
        return pltpu.make_async_copy(accw.at[:, pl.ds((i - 1) * 2 * fb, fb)], (own_g, own_u)[i - 1], o_l.at[i])

    def rs_hop(j, d, z):
        a, b = lax.rem(j, 2), lax.rem(j + 1, S)
        return remote(rso.at[a, d, z], rsb.at[b, d, z], rs_s.at[a, d, z], rs_r.at[b, d, z], down[d])

    def part_hop(j):
        b = lax.rem(j, 2)
        return remote(sout.at[b], sin.at[b], p_s.at[b], p_r.at[b], sib)

    barrier = pltpu.get_barrier_semaphore()
    for dev in down + [sib, mates[0][0], mates[1][0]]:
        pl.semaphore_signal(barrier, inc=1, device_id={"tp": dev}, device_id_type=MESH)
    for i in range(3):
        w_local(i).start()
    pl.semaphore_wait(barrier, 5)
    for d in range(2):
        ring(0, 0, d, True).start()
    for k in range(2):
        w_remote(0, k).start()
    for d in range(2):
        ring(1, 0, d, True).start()
    for d in range(2):
        cross(0, 0, d, True).start()
    lax.fori_loop(0, m, u_send, 0)
    for d in range(2):
        cross(1, 0, d, True).start()
    for i in (1, 2):
        for k in range(2):
            w_remote(i, k).start()

    def zero(i, _):
        accd[pl.ds(pl.multiple_of(i * (2 * fb // 8), 2 * fb // 8), 2 * fb // 8), :] = jnp.zeros((2 * fb // 8, h), F32)
        accw[pl.ds(pl.multiple_of(i * (h // 8), h // 8), h // 8), :] = jnp.zeros((h // 8, 4 * fb), F32)
        return 0

    lax.fori_loop(0, 8, zero, 0)

    ct = min(512, h)
    ht = min(256, h)

    def forward(i, v):
        @pl.when((v >= 1) & (v < m))
        def _():
            for d in range(2):
                ring(i, v - 1, d).wait_recv()

                @pl.when(v < m - 1)
                def _(d=d):
                    ring(i, v, d).start()

                cross(i, v, d).start()

    def count(v):
        return jnp.maximum(jnp.minimum(v + jnp.where(v >= 3, 1, 0), m), 0)

    def grads(t, hi):
        b = lax.rem(t, 2)

        @pl.when(t + 1 < hi)
        def _():
            tile_load(0, t + 1)

        @pl.when(t == 0)
        def _():
            w_local(0).wait()
            for k in range(2):
                w_remote(0, k).wait_recv()

        for k in range(2):
            u_all(t, k).wait_recv()
        pltpu.make_async_copy(uo.at[b], uo.at[b], u_l.at[b]).wait()
        tile_wait(0, t)
        for f in range(2):
            gbuf[:, f * fb:(f + 1) * fb] = dot(dyt[b].reshape(2 * tb, h), wdb[f * fb:(f + 1) * fb, :], 1, 1)

        def act(r, _):
            c, d = r // 2, lax.rem(r, 2)
            rws = pl.ds(pl.multiple_of(r * hb, hb), hb)
            half = pl.ds(pl.multiple_of(d * hb, hb), hb)
            for lo, n, get in (
                (0, fb, lambda j: uo[b, j, c, d]),
                (fb, fh, lambda j: ux[t, 0, j, c, d]),
                (fb + fh, fh, lambda j: ux[t, 1, j, c, d]),
            ):
                g = gbuf[rws, lo:lo + n]
                ug = get(0).astype(F32)
                uu = get(1).astype(F32)
                sg = jax.nn.sigmoid(ug)
                a = ug * sg
                zb[rws, lo:lo + n] = (a * uu).astype(BF16)
                dub[t, c, half, lo:lo + n] = (g * uu * sg * (1.0 + ug * (1.0 - sg))).astype(BF16)
                dub[t, c, half, 2 * fb + lo:2 * fb + lo + n] = (g * a).astype(BF16)
            return 0

        lax.fori_loop(0, 4, act, 0)

        def dwd_tile(j, _):
            cols = pl.ds(pl.multiple_of(j * ct, ct), ct)
            accd[:, cols] += dot(zb[...], dyt[b, :, :, :, cols].reshape(2 * tb, ct), 0, 0)
            return 0

        lax.fori_loop(0, h // ct, dwd_tile, 0)

    def weight_grads(t, hi):
        b = lax.rem(t, 2)

        @pl.when(t + 1 < hi)
        def _():
            tile_load(1, t + 1)

        tile_wait(1, t)

        def dw_tile(j, _):
            cols = pl.ds(pl.multiple_of(j * ht, ht), ht)
            accw[cols, :] += dot(xt[b, :, :, :, cols].reshape(2 * tb, ht), dub[t].reshape(2 * tb, 4 * fb), 0, 0)
            return 0

        lax.fori_loop(0, h // ht, dw_tile, 0)

    def partial(j):
        t = lax.rem(j, m)
        b = lax.rem(j, 2)

        @pl.when(j >= 3)
        def _():
            part_hop(j - 2).wait_send()

        def send_tile(c, _):
            cols = pl.ds(pl.multiple_of(c * ct, ct), ct)
            sout[b, :, cols] = dot(dub[t, other], wgu[cols, :], 1, 1).astype(BF16)
            return 0

        lax.fori_loop(0, h // ct, send_tile, 0)

        def keep_tile(c, _):
            cols = pl.ds(pl.multiple_of(c * ct, ct), ct)
            pbuf[:, cols] = dot(dub[t, core], wgu[cols, :], 1, 1)
            return 0

        lax.fori_loop(0, h // ct, keep_tile, 0)
        part_hop(j).start()

    def total(j, d, z, first):
        lo = pl.multiple_of(d * hb + z * q4, q4)
        v = pbuf[pl.ds(lo, q4), :] + sin[lax.rem(j, 2), pl.ds(lo, q4), :].astype(F32)
        if not first:
            v = v + rsb[lax.rem(j, S), d, z].astype(F32)
        return v.astype(BF16)

    def step(v, _):
        a0, a1 = count(v - 1), count(v)
        c0, c1 = count(v - 2), a0
        forward(0, v)

        @pl.when(a0 < a1)
        def _():
            tile_load(0, a0)

        def c_body(t, _):
            weight_grads(t, c1)
            return 0

        lax.fori_loop(c0, c1, c_body, 0)
        forward(1, v)

        @pl.when(a0 < a1)
        def _():
            tile_load(1, a0)

        def a_body(t, _):
            grads(t, a1)
            return 0

        lax.fori_loop(a0, a1, a_body, 0)

        @pl.when(v == m - 1)
        def _():
            for k in range(2):
                swap(0, k).start()
            own_out(0).start()

        @pl.when(v == m)
        def _():
            for i in (1, 2):
                for k in range(2):
                    swap(i, k).start()
                own_out(i).start()

        j = v - (m - 3)

        @pl.when(j >= 1)
        def _():
            part_hop(j).wait_recv()

            @pl.when(j >= 3)
            def _():
                for d in range(2):
                    for z in range(2):
                        rs_hop(j - 2, d, z).wait_send()

            for z in range(2):
                @pl.when(j >= 2)
                def _(z=z):
                    for d in range(2):
                        rs_hop(j - 1, d, z).wait_recv()
                        rso[lax.rem(j, 2), d, z] = total(j, d, z, False)

                @pl.when(j == 1)
                def _(z=z):
                    for d in range(2):
                        rso[lax.rem(j, 2), d, z] = total(j, d, z, True)

                for d in range(2):
                    rs_hop(j, d, z).start()

        @pl.when(j == 0)
        def _():
            for i in (1, 2):
                w_local(i).wait()
                for k in range(2):
                    w_remote(i, k).wait_recv()

        @pl.when(j >= 0)
        def _():
            partial(j + 1)

        return 0

    lax.fori_loop(0, 2 * m - 3, step, 0)

    part_hop(m).wait_recv()
    outs = []
    for d in range(2):
        for z in range(2):
            rs_hop(m - 2, d, z).wait_send()
    for z in range(2):
        for d in range(2):
            rs_hop(m - 1, d, z).wait_recv()
            rso[m % 2, d, z] = total(m, d, z, False)
            outs.append(pltpu.make_async_copy(rso.at[m % 2, d, z], dx_h.at[pl.ds(d * hb + z * q4, q4)], o_l.at[3 + 2 * d + z]))
            outs[-1].start()

    for i in range(3):
        own_out(i).wait()
        for k in range(2):
            swap(i, k).wait()
            w_remote(i, k).wait_send()
    for j in (m - 1, m):
        part_hop(j).wait_send()
    for d in range(2):
        for z in range(2):
            rs_hop(m - 1, d, z).wait_send()

    def drain(s, _):
        for k in range(2):
            u_all(s, k).wait_send()
        for i in range(2):
            for d in range(2):
                cross(i, s, d).wait_send()

                @pl.when(s < m - 1)
                def _(i=i, d=d):
                    ring(i, s, d).wait_send()
        return 0

    lax.fori_loop(0, m, drain, 0)
    for c in outs:
        c.wait()


def solution(mesh):
    tok = P(("dp", "tp"), None)
    col = P(None, "tp")
    row = P("tp", None)
    act = P("dp", "tp")
    n = mesh.shape["tp"] // 2
    side = math.isqrt(n)
    m = 2 * side

    def body(x, dy, wg, wu, wd, ug, uu):
        tb, h = x.shape
        fb = wg.shape[1]
        hb, fh = tb // 2, fb // 2
        vm = pltpu.VMEM
        dma = pltpu.SemaphoreType.DMA
        sds = jax.ShapeDtypeStruct
        flops = 12 * n * tb * h * 2 * fb
        dx, own_d, own_g, own_u, rec_d, rec_g, rec_u, _, _ = pl.pallas_call(
            functools.partial(kernel, side),
            out_shape=(
                sds((tb, h), BF16),
                sds((fb, h), F32), sds((h, fb), F32), sds((h, fb), F32),
                sds((fb, h), F32), sds((h, fb), F32), sds((h, fb), F32),
                sds((m, 2, 2, hb, h), BF16), sds((m, 2, 2, hb, h), BF16),
            ),
            in_specs=[pl.BlockSpec(memory_space=pl.ANY)] * 7,
            out_specs=[pl.BlockSpec(memory_space=pl.ANY)] * 9,
            scratch_shapes=[
                vm((2, 2, 2, hb, h), BF16),
                vm((2, 2, 2, hb, h), BF16),
                vm((2, 2, 2, 2, hb, fb), BF16),
                vm((m, 2, 2, 2, 2, hb, fh), BF16),
                vm((2 * fb, h), BF16),
                vm((h, 4 * fb), BF16),
                vm((2 * tb, 2 * fb), F32),
                vm((2 * tb, 2 * fb), BF16),
                vm((m, 2, tb, 4 * fb), BF16),
                vm((2 * fb, h), F32),
                vm((h, 4 * fb), F32),
                vm((tb, h), F32),
                vm((2, tb, h), BF16),
                vm((2, tb, h), BF16),
                vm((S, 2, 2, hb // 2, h), BF16),
                vm((2, 2, 2, hb // 2, h), BF16),
                dma((m, 2)), dma((m, 2)), dma((m, 2)), dma((m, 2)),
                dma((m, 2)), dma((m, 2)), dma((m, 2)), dma((m, 2)),
                dma((2,)), dma((2,)), dma((m, 2)), dma((m, 2)), dma((2,)),
                dma((3, 2)), dma((3, 2)), dma((3,)), dma((2,)), dma((2,)),
                dma((2, 2, 2)), dma((S, 2, 2)), dma((3, 2)), dma((3, 2)), dma((7,)),
            ],
            compiler_params=pltpu.CompilerParams(
                collective_id=0, has_side_effects=True, vmem_limit_bytes=62 * 1024 * 1024
            ),
            cost_estimate=pl.CostEstimate(flops=flops, bytes_accessed=2 * flops // 1000, transcendentals=0),
        )(
            x.reshape(2, hb, h), dy.reshape(2, hb, h), wg, wu, wd,
            ug.reshape(n, 2, 2, hb, fb), uu.reshape(n, 2, 2, hb, fb),
        )
        return dx, own_g + rec_g, own_u + rec_u, own_d + rec_d

    return jax.shard_map(
        body, mesh=mesh, in_specs=(tok, tok, col, col, row, act, act), out_specs=(tok, act, act, tok), check_vma=False
    )
```

time: 398 us -> 256 us (0.64)
  Pallas kernels: 0 us -> 246 us
  waiting for transfers between devices: 239 us -> 0 us
  matrix products: 141 us -> 0 us
  between operations: 13.8 us -> 0.67 us
  other arithmetic: 0 us -> 7.14 us
    pallas_call x0 -> x1, Pallas kernels: none -> 246 us  [body(): pl.pallas_call(functools.partial(kernel, side), out_shape=(sds((tb, h), B...]
    dot_general x6 -> x0, matrix products: 141 us -> none  [the longest x1 38.2 us: body(): jnp.dot(duu, wu.T, preferred_element_type=jnp.float32)]
    all_gather x2 -> x0, waiting for transfers between devices: 136 us -> none  [the longest x1 114 us: body(): dyg = lax.all_gather(dy, 'tp', axis=0, tiled=True)]
    reduce_scatter x1 -> x0, waiting for transfers between devices: 101 us -> none  [body(): lax.psum_scatter(p.astype(jnp.bfloat16), 'tp', scatter_dimension=0, tiled...]
    add x0 -> x3, other arithmetic: none -> 7.14 us  [body(): return (dx, own_g + rec_g, own_u + rec_u, own_d + rec_d)]
  transfers between devices with their start and end apart: 3 -> 0, of which waited for: 3 -> 0; matrix products, arithmetic and copies ran while one was open for 36% -> 0% of each run, Pallas kernels for 0% -> 0%
where the time goes in v2:
time: 256 us
  Pallas kernels  246 us (96%)
  other arithmetic  7.14 us (3%)
    pallas_call x1, Pallas kernels, body(): pl.pallas_call(functools.partial(kernel, side), out_shape=(sds((tb, h), B...  246 us
    add x3, other arithmetic, body(): return (dx, own_g + rec_g, own_u + rec_u, own_d + rec_d)  7.14 us

profile of v2, /device:TPU:97, one launch (start us, length us, event | category | flops | bytes accessed | tf_op | source)
XLA Modules:
  0.0 255.8 jit_solution(6310579842867935788)
XLA Ops:
  0.6 245.6 %shard_map.102 = (bf16[256,2048]{1,0:T(8,128)(2,1)}, f32[256,2048]{1,0:T(8,128)}, f32[2048,256]{1,0:T(8,128)}, f32[2048,256]{1,0:T(8,128)}, f32[256,2048]{1,0:T(...) custom-call(bf16[2,128,2048]{2,1,0:T(8,128)(2,1)} %bitcast.6, ...), custom_call_target="tpu_custom_call" | custom-call | flops 51539607552 | bytes 103079216 | tf_op jit(solution)/shard_map/pallas_call | solution.py:432
  246.2 0.0 copy-start.2
  246.3 0.0 copy-start.3
  246.3 4.0 %add.9 = f32[2048,256]{1,0:T(8,128)} add(f32[2048,256]{1,0:T(8,128)} %get-tuple-element.12, f32[2048,256]{1,0:T(8,128)} %get-tuple-element.13) | non-fusion elementwise | flops 524288 | bytes 6291456 | tf_op jit(solution)/shard_map/add | solution.py:473
  250.2 0.0 copy-done.2
  250.3 0.0 copy-done.3
  250.3 0.0 copy-start
  250.3 0.0 copy-start.1
  250.3 1.6 add.10
  251.9 0.7 copy-done
  252.6 0.6 copy-done.1
  253.2 0.0 copy-start.4
  253.2 1.6 add.11
  254.8 0.0 copy-done.4
  254.8 1.0 copy.12
Async XLA Ops:
  246.2 4.0 %copy-start.2 = (f32[2048,256]{1,0:T(8,128)S(1)}, f32[2048,256]{1,0:T(8,128)}, u32[]{:S(2)}) copy-start(f32[2048,256]{1,0:T(8,128)} %get-tuple-element.14) | copy-start | bytes 6291460
  246.3 4.0 %copy-start.3 = (f32[2048,256]{1,0:T(8,128)S(1)}, f32[2048,256]{1,0:T(8,128)}, u32[]{:S(2)}) copy-start(f32[2048,256]{1,0:T(8,128)} %get-tuple-element.15) | copy-start | bytes 6291460
  250.3 2.3 copy-start
  250.3 3.0 %copy-start.1 = (f32[256,2048]{1,0:T(8,128)S(1)}, f32[256,2048]{1,0:T(8,128)}, u32[]{:S(2)}) copy-start(f32[256,2048]{1,0:T(8,128)} %get-tuple-element.17) | copy-start | bytes 6291460
  253.2 1.6 copy-start.4

commit v3 on v2

--- a/solution.py
+++ b/solution.py
@@ -21,10 +21,10 @@
 def kernel(
     side,
     x_h, dy_h, wg_h, wu_h, wd_h, ug_h, uu_h,
-    dx_h, own_d, own_g, own_u, rec_d, rec_g, rec_u, dyl, xl,
+    dx_h, own_d, own_g, own_u, rec_d, rec_g, rec_u, dyl, xl, rl,
     dyt, xt, uo, ux, wdb, wgu, gbuf, zb, dub, accd, accw, pbuf, sin, sout, rsb, rso,
     dyr_s, dyr_r, dyc_s, dyc_r, xr_s, xr_r, xc_s, xc_r, dyt_l, xt_l, u_s, u_r, u_l,
-    w_s, w_r, w_l, p_s, p_r, rs_s, rs_r, e_s, e_r, o_l,
+    w_s, w_r, w_l, p_s, p_r, rs_s, rs_r, e_s, e_r, o_l, b_s, b_r, l_s,
 ):
     _, hb, h = dy_h.shape
     tb = 2 * hb
@@ -61,6 +61,8 @@
         c = lax.rem(x + y, side)
         mates.append(((y * side + x) * 2 + core, c // 2, ring_pos(y, lax.rem(c, 2))))
 
+    leave = [jnp.where(odd == d, mates[1][0], mates[0][0]) for d in range(2)]
+
     def remote(src, dst, ss, rs, dev):
         return pltpu.make_async_remote_copy(
             src_ref=src, dst_ref=dst, send_sem=ss, recv_sem=rs, device_id={"tp": dev}, device_id_type=MESH
@@ -71,6 +73,12 @@
     def ring(i, s, d, first=False):
         src, land, ss, rs = rows[i][:4]
         return remote(src.at[d] if first else land.at[s, core, d], land.at[s + 1, core, d], ss.at[s, d], rs.at[s + 1, d], down[d])
+
+    def away(k, d, first=False):
+        return remote(x_h.at[d] if first else xl.at[2 * k, core, d], rl.at[k, d], b_s.at[k, d], b_r.at[k, d], leave[d])
+
+    def relay(k, d):
+        return remote(rl.at[k, d], xl.at[2 * k + 2, core, d], l_s.at[k, d], xr_r.at[2 * k + 2, d], leave[d])
 
     def cross(i, s, d, first=False):
         src, land, ss, rs = rows[i][0], rows[i][1], rows[i][4], rows[i][5]
@@ -159,18 +167,17 @@
     pl.semaphore_wait(barrier, 5)
     for d in range(2):
         ring(0, 0, d, True).start()
+        away(0, d, True).start()
     for k in range(2):
         w_remote(0, k).start()
     for d in range(2):
         ring(1, 0, d, True).start()
     for d in range(2):
         cross(0, 0, d, True).start()
-    lax.fori_loop(0, m, u_send, 0)
+    u_send(0, 0)
+    u_send(1, 0)
     for d in range(2):
         cross(1, 0, d, True).start()
-    for i in (1, 2):
-        for k in range(2):
-            w_remote(i, k).start()
 
     def zero(i, _):
         accd[pl.ds(pl.multiple_of(i * (2 * fb // 8), 2 * fb // 8), 2 * fb // 8), :] = jnp.zeros((2 * fb // 8, h), F32)
@@ -182,17 +189,44 @@
     ct = min(512, h)
     ht = min(256, h)
 
-    def forward(i, v):
+    def forward_dy(v):
         @pl.when((v >= 1) & (v < m))
         def _():
             for d in range(2):
-                ring(i, v - 1, d).wait_recv()
+                ring(0, v - 1, d).wait_recv()
 
                 @pl.when(v < m - 1)
                 def _(d=d):
-                    ring(i, v, d).start()
-
-                cross(i, v, d).start()
+                    ring(0, v, d).start()
+
+                cross(0, v, d).start()
+
+    def forward_x(v):
+        k = v // 2
+
+        @pl.when((v >= 1) & (v < m) & (lax.rem(v, 2) == 1))
+        def _():
+            @pl.when(v < m - 1)
+            def _():
+                for d in range(2):
+                    away(k, d).wait_recv()
+                    relay(k, d).start()
+
+            for d in range(2):
+                ring(1, v - 1, d).wait_recv()
+                cross(1, v, d).start()
+
+        @pl.when((v >= 1) & (v < m) & (lax.rem(v, 2) == 0))
+        def _():
+            for d in range(2):
+                relay(k - 1, d).wait_recv()
+
+                @pl.when(v < m - 2)
+                def _(d=d):
+                    away(k, d).start()
+
+                ring(1, v, d).start()
+                cross(1, v, d).start()
 
     def count(v):
         return jnp.maximum(jnp.minimum(v + jnp.where(v >= 3, 1, 0), m), 0)
@@ -293,8 +327,8 @@
 
     def step(v, _):
         a0, a1 = count(v - 1), count(v)
-        c0, c1 = count(v - 2), a0
-        forward(0, v)
+        c0, c1 = count(v - 2), jnp.minimum(a0, m - 1)
+        forward_dy(v)
 
         @pl.when(a0 < a1)
         def _():
@@ -305,7 +339,17 @@
             return 0
 
         lax.fori_loop(c0, c1, c_body, 0)
-        forward(1, v)
+        forward_x(v)
+
+        @pl.when(v + 2 < m)
+        def _():
+            u_send(v + 2, 0)
+
+        for i in (1, 2):
+            @pl.when(v == i)
+            def _(i=i):
+                for k in range(2):
+                    w_remote(i, k).start()
 
         @pl.when(a0 < a1)
         def _():
@@ -322,15 +366,13 @@
             for k in range(2):
                 swap(0, k).start()
             own_out(0).start()
-
-        @pl.when(v == m)
-        def _():
+            weight_grads(v, m)
             for i in (1, 2):
                 for k in range(2):
                     swap(i, k).start()
                 own_out(i).start()
 
-        j = v - (m - 3)
+        j = v - (m - 4)
 
         @pl.when(j >= 1)
         def _():
@@ -370,7 +412,7 @@
 
         return 0
 
-    lax.fori_loop(0, 2 * m - 3, step, 0)
+    lax.fori_loop(0, 2 * m - 4, step, 0)
 
     part_hop(m).wait_recv()
     outs = []
@@ -402,12 +444,16 @@
             for d in range(2):
                 cross(i, s, d).wait_send()
 
-                @pl.when(s < m - 1)
+                @pl.when(s < m - 1 if i == 0 else lax.rem(s, 2) == 0)
                 def _(i=i, d=d):
                     ring(i, s, d).wait_send()
         return 0
 
     lax.fori_loop(0, m, drain, 0)
+    for k in range(side - 1):
+        for d in range(2):
+            away(k, d).wait_send()
+            relay(k, d).wait_send()
     for c in outs:
         c.wait()
 
@@ -429,16 +475,16 @@
         dma = pltpu.SemaphoreType.DMA
         sds = jax.ShapeDtypeStruct
         flops = 12 * n * tb * h * 2 * fb
-        dx, own_d, own_g, own_u, rec_d, rec_g, rec_u, _, _ = pl.pallas_call(
+        dx, own_d, own_g, own_u, rec_d, rec_g, rec_u, _, _, _ = pl.pallas_call(
             functools.partial(kernel, side),
             out_shape=(
                 sds((tb, h), BF16),
                 sds((fb, h), F32), sds((h, fb), F32), sds((h, fb), F32),
                 sds((fb, h), F32), sds((h, fb), F32), sds((h, fb), F32),
-                sds((m, 2, 2, hb, h), BF16), sds((m, 2, 2, hb, h), BF16),
+                sds((m, 2, 2, hb, h), BF16), sds((m, 2, 2, hb, h), BF16), sds((side - 1, 2, hb, h), BF16),
             ),
-            in_specs=[pl.BlockSpec(memory_space=pl.ANY)] * 7,
-            out_specs=[pl.BlockSpec(memory_space=pl.ANY)] * 9,
+            in_specs=[pl.BlockSpec(memory_space=pltpu.HBM)] * 7,
+            out_specs=[pl.BlockSpec(memory_space=pl.ANY)] * 10,
             scratch_shapes=[
                 vm((2, 2, 2, hb, h), BF16),
                 vm((2, 2, 2, hb, h), BF16),
@@ -461,6 +507,7 @@
                 dma((2,)), dma((2,)), dma((m, 2)), dma((m, 2)), dma((2,)),
                 dma((3, 2)), dma((3, 2)), dma((3,)), dma((2,)), dma((2,)),
                 dma((2, 2, 2)), dma((S, 2, 2)), dma((3, 2)), dma((3, 2)), dma((7,)),
+                dma((side - 1, 2)), dma((side - 1, 2)), dma((side - 1, 2)),
             ],
             compiler_params=pltpu.CompilerParams(
                 collective_id=0, has_side_effects=True, vmem_limit_bytes=62 * 1024 * 1024

time: 256 us -> 261 us (1.020)
  Pallas kernels: 246 us -> 251 us
    pallas_call x1, Pallas kernels: 246 us -> 251 us  [body(): pl.pallas_call(functools.partial(kernel, side), out_shape=(sds((tb, h), B...]
where the time goes in v3:
time: 261 us
  Pallas kernels  251 us (96%)
  other arithmetic  7.14 us (3%)
    pallas_call x1, Pallas kernels, body(): pl.pallas_call(functools.partial(kernel, side), out_shape=(sds((tb, h), B...  251 us
    add x3, other arithmetic, body(): return (dx, own_g + rec_g, own_u + rec_u, own_d + rec_d)  7.14 us

profile of v3, /device:TPU:97, one launch (start us, length us, event | category | flops | bytes accessed | tf_op | source)
XLA Modules:
  0.0 261.0 jit_solution(9186108122831282273)
XLA Ops:
  0.6 250.8 %shard_map.102 = (bf16[256,2048]{1,0:T(8,128)(2,1)}, f32[256,2048]{1,0:T(8,128)}, f32[2048,256]{1,0:T(8,128)}, f32[2048,256]{1,0:T(8,128)}, f32[256,2048]{1,0:T(...) custom-call(bf16[2,128,2048]{2,1,0:T(8,128)(2,1)} %bitcast.6, ...), custom_call_target="tpu_custom_call" | custom-call | flops 51539607552 | bytes 103079216 | tf_op jit(solution)/shard_map/pallas_call | solution.py:478
  251.4 0.0 copy-start.2
  251.4 0.0 copy-start.3
  251.5 4.0 %add.9 = f32[2048,256]{1,0:T(8,128)} add(f32[2048,256]{1,0:T(8,128)} %get-tuple-element.12, f32[2048,256]{1,0:T(8,128)} %get-tuple-element.13) | non-fusion elementwise | flops 524288 | bytes 6291456 | tf_op jit(solution)/shard_map/add | solution.py:520
  255.4 0.0 copy-done.2
  255.4 0.0 copy-done.3
  255.4 0.0 copy-start
  255.4 0.0 copy-start.1
  255.5 1.6 add.10
  257.0 0.7 copy-done
  257.8 0.6 copy-done.1
  258.4 0.0 copy-start.4
  258.4 1.6 add.11
  260.0 0.0 copy-done.4
  260.0 1.0 copy.12
Async XLA Ops:
  251.4 4.0 %copy-start.2 = (f32[2048,256]{1,0:T(8,128)S(1)}, f32[2048,256]{1,0:T(8,128)}, u32[]{:S(2)}) copy-start(f32[2048,256]{1,0:T(8,128)} %get-tuple-element.14) | copy-start | bytes 6291460
  251.4 4.0 %copy-start.3 = (f32[2048,256]{1,0:T(8,128)S(1)}, f32[2048,256]{1,0:T(8,128)}, u32[]{:S(2)}) copy-start(f32[2048,256]{1,0:T(8,128)} %get-tuple-element.15) | copy-start | bytes 6291460
  255.4 2.3 copy-start
  255.4 3.0 %copy-start.1 = (f32[256,2048]{1,0:T(8,128)S(1)}, f32[256,2048]{1,0:T(8,128)}, u32[]{:S(2)}) copy-start(f32[256,2048]{1,0:T(8,128)} %get-tuple-element.17) | copy-start | bytes 6291460
  258.4 1.6 copy-start.4

commit v4 on v2

--- a/solution.py
+++ b/solution.py
@@ -12,6 +12,14 @@
 BF16 = jnp.bfloat16
 S = 4
 MESH = pl.DeviceIdType.MESH
+PLAN = (
+    "W0", "a0", "c0", "U0", "Y1", "L0", "a1", "O1", "c1", "U1", "A0", "C0", "U2", "Y2", "U3", "a2", "E2",
+    "c2", "A1", "C1", "Y3", "A2", "W1", "a3", "C2", "A3", "O3", "W2", "L1", "c3", "C3", "Y4", "a4", "Y5",
+    "U4", "P1", "a5", "P2", "U5", "R2", "R3", "P3", "U6", "E4", "Y6", "c4", "A4", "R4", "a6", "C4", "R5",
+    "P4", "U7", "A5", "A6", "O5", "L2", "c5", "C5", "Y7", "a7", "A7", "S0", "E6", "R6", "R7", "c6", "P5",
+    "C6", "O7", "c7", "C7", "S1", "R8", "R9", "P6", "R10", "R11", "P7", "R12", "R13", "P8", "R14", "R15",
+)
+KINDS = "YLEOacACPRSUW"
 
 
 def dot(a, b, ca, cb):
@@ -21,10 +29,10 @@
 def kernel(
     side,
     x_h, dy_h, wg_h, wu_h, wd_h, ug_h, uu_h,
-    dx_h, own_d, own_g, own_u, rec_d, rec_g, rec_u, dyl, xl,
+    dx_h, own_d, own_g, own_u, rec_d, rec_g, rec_u, dyl, xl, rl,
     dyt, xt, uo, ux, wdb, wgu, gbuf, zb, dub, accd, accw, pbuf, sin, sout, rsb, rso,
     dyr_s, dyr_r, dyc_s, dyc_r, xr_s, xr_r, xc_s, xc_r, dyt_l, xt_l, u_s, u_r, u_l,
-    w_s, w_r, w_l, p_s, p_r, rs_s, rs_r, e_s, e_r, o_l,
+    w_s, w_r, w_l, p_s, p_r, rs_s, rs_r, e_s, e_r, o_l, b_s, b_r, l_s,
 ):
     _, hb, h = dy_h.shape
     tb = 2 * hb
@@ -61,6 +69,8 @@
         c = lax.rem(x + y, side)
         mates.append(((y * side + x) * 2 + core, c // 2, ring_pos(y, lax.rem(c, 2))))
 
+    leave = [jnp.where(odd == d, mates[1][0], mates[0][0]) for d in range(2)]
+
     def remote(src, dst, ss, rs, dev):
         return pltpu.make_async_remote_copy(
             src_ref=src, dst_ref=dst, send_sem=ss, recv_sem=rs, device_id={"tp": dev}, device_id_type=MESH
@@ -72,6 +82,12 @@
         src, land, ss, rs = rows[i][:4]
         return remote(src.at[d] if first else land.at[s, core, d], land.at[s + 1, core, d], ss.at[s, d], rs.at[s + 1, d], down[d])
 
+    def away(k, d, first=False):
+        return remote(x_h.at[d] if first else xl.at[2 * k, core, d], rl.at[k, d], b_s.at[k, d], b_r.at[k, d], leave[d])
+
+    def relay(k, d):
+        return remote(rl.at[k, d], xl.at[2 * k + 2, core, d], l_s.at[k, d], xr_r.at[2 * k + 2, d], leave[d])
+
     def cross(i, s, d, first=False):
         src, land, ss, rs = rows[i][0], rows[i][1], rows[i][4], rows[i][5]
         return remote(src.at[d] if first else land.at[s, core, d], land.at[s, core, d], ss.at[s, d], rs.at[s, d], sib)
@@ -106,13 +122,12 @@
                 for j, u in enumerate((ug_h, uu_h)):
                     pltpu.make_async_copy(u.at[o, :, d], uo.at[b, j, :, d], u_l.at[b]).start()
 
-    def u_send(t, _):
+    def u_send(t):
         for k, (dev, g, p) in enumerate(mates):
             for d in range(2):
                 o = origin(g, p, d, t)
                 for j, u in enumerate((ug_h, uu_h)):
                     remote(u.at[o, :, d, :, pl.ds(k * fh, fh)], ux.at[t, k, j, :, d], u_s.at[t, k], u_r.at[t, k], dev).start()
-        return 0
 
     def u_all(t, k):
         return remote(ux.at[t, k], ux.at[t, k], u_s.at[t, k], u_r.at[t, k], mates[k][0])
@@ -148,8 +163,8 @@
         return remote(rso.at[a, d, z], rsb.at[b, d, z], rs_s.at[a, d, z], rs_r.at[b, d, z], down[d])
 
     def part_hop(j):
-        b = lax.rem(j, 2)
-        return remote(sout.at[b], sin.at[b], p_s.at[b], p_r.at[b], sib)
+        a, b = lax.rem(j, 2), lax.rem(j, S)
+        return remote(sout.at[a], sin.at[b], p_s.at[a], p_r.at[b], sib)
 
     barrier = pltpu.get_barrier_semaphore()
     for dev in down + [sib, mates[0][0], mates[1][0]]:
@@ -159,18 +174,11 @@
     pl.semaphore_wait(barrier, 5)
     for d in range(2):
         ring(0, 0, d, True).start()
-    for k in range(2):
-        w_remote(0, k).start()
+        away(0, d, True).start()
     for d in range(2):
         ring(1, 0, d, True).start()
-    for d in range(2):
         cross(0, 0, d, True).start()
-    lax.fori_loop(0, m, u_send, 0)
-    for d in range(2):
         cross(1, 0, d, True).start()
-    for i in (1, 2):
-        for k in range(2):
-            w_remote(i, k).start()
 
     def zero(i, _):
         accd[pl.ds(pl.multiple_of(i * (2 * fb // 8), 2 * fb // 8), 2 * fb // 8), :] = jnp.zeros((2 * fb // 8, h), F32)
@@ -182,27 +190,40 @@
     ct = min(512, h)
     ht = min(256, h)
 
-    def forward(i, v):
-        @pl.when((v >= 1) & (v < m))
-        def _():
-            for d in range(2):
-                ring(i, v - 1, d).wait_recv()
-
-                @pl.when(v < m - 1)
-                def _(d=d):
-                    ring(i, v, d).start()
-
-                cross(i, v, d).start()
-
-    def count(v):
-        return jnp.maximum(jnp.minimum(v + jnp.where(v >= 3, 1, 0), m), 0)
-
-    def grads(t, hi):
+    def pass_dy(s):
+        for d in range(2):
+            ring(0, s - 1, d).wait_recv()
+
+            @pl.when(s < m - 1)
+            def _(d=d):
+                ring(0, s, d).start()
+
+            cross(0, s, d).start()
+
+    def relay_x(k):
+        for d in range(2):
+            away(k, d).wait_recv()
+            relay(k, d).start()
+
+    def pass_even_x(s):
+        k = s // 2
+        for d in range(2):
+            relay(k - 1, d).wait_recv()
+
+            @pl.when(s < m - 2)
+            def _(d=d):
+                away(k, d).start()
+
+            ring(1, s, d).start()
+            cross(1, s, d).start()
+
+    def take_odd_x(s):
+        for d in range(2):
+            ring(1, s - 1, d).wait_recv()
+            cross(1, s, d).start()
+
+    def grads(t):
         b = lax.rem(t, 2)
-
-        @pl.when(t + 1 < hi)
-        def _():
-            tile_load(0, t + 1)
 
         @pl.when(t == 0)
         def _():
@@ -245,12 +266,8 @@
 
         lax.fori_loop(0, h // ct, dwd_tile, 0)
 
-    def weight_grads(t, hi):
+    def weight_grads(t):
         b = lax.rem(t, 2)
-
-        @pl.when(t + 1 < hi)
-        def _():
-            tile_load(1, t + 1)
 
         tile_wait(1, t)
 
@@ -265,6 +282,13 @@
         t = lax.rem(j, m)
         b = lax.rem(j, 2)
 
+        @pl.when(j == 1)
+        def _():
+            for i in (1, 2):
+                w_local(i).wait()
+                for k in range(2):
+                    w_remote(i, k).wait_recv()
+
         @pl.when(j >= 3)
         def _():
             part_hop(j - 2).wait_send()
@@ -278,7 +302,7 @@
 
         def keep_tile(c, _):
             cols = pl.ds(pl.multiple_of(c * ct, ct), ct)
-            pbuf[:, cols] = dot(dub[t, core], wgu[cols, :], 1, 1)
+            pbuf[b, :, cols] = dot(dub[t, core], wgu[cols, :], 1, 1)
             return 0
 
         lax.fori_loop(0, h // ct, keep_tile, 0)
@@ -286,91 +310,71 @@
 
     def total(j, d, z, first):
         lo = pl.multiple_of(d * hb + z * q4, q4)
-        v = pbuf[pl.ds(lo, q4), :] + sin[lax.rem(j, 2), pl.ds(lo, q4), :].astype(F32)
+        v = pbuf[lax.rem(j, 2), pl.ds(lo, q4), :] + sin[lax.rem(j, S), pl.ds(lo, q4), :].astype(F32)
         if not first:
             v = v + rsb[lax.rem(j, S), d, z].astype(F32)
         return v.astype(BF16)
 
-    def step(v, _):
-        a0, a1 = count(v - 1), count(v)
-        c0, c1 = count(v - 2), a0
-        forward(0, v)
-
-        @pl.when(a0 < a1)
-        def _():
-            tile_load(0, a0)
-
-        def c_body(t, _):
-            weight_grads(t, c1)
-            return 0
-
-        lax.fori_loop(c0, c1, c_body, 0)
-        forward(1, v)
-
-        @pl.when(a0 < a1)
-        def _():
-            tile_load(1, a0)
-
-        def a_body(t, _):
-            grads(t, a1)
-            return 0
-
-        lax.fori_loop(a0, a1, a_body, 0)
-
-        @pl.when(v == m - 1)
-        def _():
-            for k in range(2):
-                swap(0, k).start()
-            own_out(0).start()
-
-        @pl.when(v == m)
-        def _():
-            for i in (1, 2):
+    def pass_sum(i):
+        j, z = i // 2, lax.rem(i, 2)
+
+        @pl.when(z == 0)
+        def _():
+            part_hop(j).wait_recv()
+
+        @pl.when(j >= 3)
+        def _():
+            for d in range(2):
+                rs_hop(j - 2, d, z).wait_send()
+
+        @pl.when(j >= 2)
+        def _():
+            for d in range(2):
+                rs_hop(j - 1, d, z).wait_recv()
+                rso[lax.rem(j, 2), d, z] = total(j, d, z, False)
+
+        @pl.when(j == 1)
+        def _():
+            for d in range(2):
+                rso[lax.rem(j, 2), d, z] = total(j, d, z, True)
+
+        for d in range(2):
+            rs_hop(j, d, z).start()
+
+    def swaps(i):
+        for which in ((0,), (1, 2)):
+            @pl.when(i == which[0])
+            def _(which=which):
+                for w in which:
+                    for k in range(2):
+                        swap(w, k).start()
+                    own_out(w).start()
+
+    def send_weight(i):
+        for w in range(3):
+            @pl.when(i == w)
+            def _(w=w):
                 for k in range(2):
-                    swap(i, k).start()
-                own_out(i).start()
-
-        j = v - (m - 3)
-
-        @pl.when(j >= 1)
-        def _():
-            part_hop(j).wait_recv()
-
-            @pl.when(j >= 3)
-            def _():
-                for d in range(2):
-                    for z in range(2):
-                        rs_hop(j - 2, d, z).wait_send()
-
-            for z in range(2):
-                @pl.when(j >= 2)
-                def _(z=z):
-                    for d in range(2):
-                        rs_hop(j - 1, d, z).wait_recv()
-                        rso[lax.rem(j, 2), d, z] = total(j, d, z, False)
-
-                @pl.when(j == 1)
-                def _(z=z):
-                    for d in range(2):
-                        rso[lax.rem(j, 2), d, z] = total(j, d, z, True)
-
-                for d in range(2):
-                    rs_hop(j, d, z).start()
-
-        @pl.when(j == 0)
-        def _():
-            for i in (1, 2):
-                w_local(i).wait()
-                for k in range(2):
-                    w_remote(i, k).wait_recv()
-
-        @pl.when(j >= 0)
-        def _():
-            partial(j + 1)
-
+                    w_remote(w, k).start()
+
+    work = dict(
+        Y=pass_dy, L=relay_x, E=pass_even_x, O=take_odd_x, a=lambda t: tile_load(0, t), c=lambda t: tile_load(1, t),
+        A=grads, C=weight_grads, P=partial, R=pass_sum, S=swaps, U=u_send, W=send_weight,
+    )
+    packed = [KINDS.index(w[0]) * 16 + int(w[1:]) for w in PLAN]
+
+    def step(i, _):
+        op = jnp.int32(packed[0])
+        for k, code in enumerate(packed[1:], 1):
+            op = jnp.where(i == k, code, op)
+        kind, arg = op // 16, lax.rem(op, 16)
+        for k, name in enumerate(KINDS):
+            @pl.when(kind == k)
+            def _(name=name):
+                work[name](arg)
         return 0
 
-    lax.fori_loop(0, 2 * m - 3, step, 0)
+    lax.fori_loop(0, len(packed), step, 0)
 
     part_hop(m).wait_recv()
     outs = []
@@ -402,12 +406,16 @@
             for d in range(2):
                 cross(i, s, d).wait_send()
 
-                @pl.when(s < m - 1)
+                @pl.when(s < m - 1 if i == 0 else lax.rem(s, 2) == 0)
                 def _(i=i, d=d):
                     ring(i, s, d).wait_send()
         return 0
 
     lax.fori_loop(0, m, drain, 0)
+    for k in range(side - 1):
+        for d in range(2):
+            away(k, d).wait_send()
+            relay(k, d).wait_send()
     for c in outs:
         c.wait()
 
@@ -429,16 +437,16 @@
         dma = pltpu.SemaphoreType.DMA
         sds = jax.ShapeDtypeStruct
         flops = 12 * n * tb * h * 2 * fb
-        dx, own_d, own_g, own_u, rec_d, rec_g, rec_u, _, _ = pl.pallas_call(
+        dx, own_d, own_g, own_u, rec_d, rec_g, rec_u, _, _, _ = pl.pallas_call(
             functools.partial(kernel, side),
             out_shape=(
                 sds((tb, h), BF16),
                 sds((fb, h), F32), sds((h, fb), F32), sds((h, fb), F32),
                 sds((fb, h), F32), sds((h, fb), F32), sds((h, fb), F32),
-                sds((m, 2, 2, hb, h), BF16), sds((m, 2, 2, hb, h), BF16),
+                sds((m, 2, 2, hb, h), BF16), sds((m, 2, 2, hb, h), BF16), sds((side - 1, 2, hb, h), BF16),
             ),
-            in_specs=[pl.BlockSpec(memory_space=pl.ANY)] * 7,
-            out_specs=[pl.BlockSpec(memory_space=pl.ANY)] * 9,
+            in_specs=[pl.BlockSpec(memory_space=pltpu.HBM)] * 7,
+            out_specs=[pl.BlockSpec(memory_space=pl.ANY)] * 10,
             scratch_shapes=[
                 vm((2, 2, 2, hb, h), BF16),
                 vm((2, 2, 2, hb, h), BF16),
@@ -451,16 +459,17 @@
                 vm((m, 2, tb, 4 * fb), BF16),
                 vm((2 * fb, h), F32),
                 vm((h, 4 * fb), F32),
-                vm((tb, h), F32),
-                vm((2, tb, h), BF16),
+                vm((2, tb, h), F32),
+                vm((S, tb, h), BF16),
                 vm((2, tb, h), BF16),
                 vm((S, 2, 2, hb // 2, h), BF16),
                 vm((2, 2, 2, hb // 2, h), BF16),
                 dma((m, 2)), dma((m, 2)), dma((m, 2)), dma((m, 2)),
                 dma((m, 2)), dma((m, 2)), dma((m, 2)), dma((m, 2)),
                 dma((2,)), dma((2,)), dma((m, 2)), dma((m, 2)), dma((2,)),
-                dma((3, 2)), dma((3, 2)), dma((3,)), dma((2,)), dma((2,)),
+                dma((3, 2)), dma((3, 2)), dma((3,)), dma((2,)), dma((S,)),
                 dma((2, 2, 2)), dma((S, 2, 2)), dma((3, 2)), dma((3, 2)), dma((7,)),
+                dma((side - 1, 2)), dma((side - 1, 2)), dma((side - 1, 2)),
             ],
             compiler_params=pltpu.CompilerParams(
                 collective_id=0, has_side_effects=True, vmem_limit_bytes=62 * 1024 * 1024

time: 256 us -> 236 us (0.922)
  Pallas kernels: 246 us -> 226 us
    pallas_call x1, Pallas kernels: 246 us -> 226 us  [body(): pl.pallas_call(functools.partial(kernel, side), out_shape=(sds((tb, h), B...]
where the time goes in v4:
time: 236 us
  Pallas kernels  226 us (96%)
  other arithmetic  7.14 us (3%)
  local copies, waits for them, and re-layouts  2.36 us (1%)
    pallas_call x1, Pallas kernels, body(): pl.pallas_call(functools.partial(kernel, side), out_shape=(sds((tb, h), B...  226 us
    add x3, other arithmetic, body(): return (dx, own_g + rec_g, own_u + rec_u, own_d + rec_d)  7.14 us

profile of v4, /device:TPU:97, one launch (start us, length us, event | category | flops | bytes accessed | tf_op | source)
XLA Modules:
  0.0 235.9 jit_solution(8404412656829057391)
XLA Ops:
  0.6 225.8 %shard_map.102 = (bf16[256,2048]{1,0:T(8,128)(2,1)}, f32[256,2048]{1,0:T(8,128)}, f32[2048,256]{1,0:T(8,128)}, f32[2048,256]{1,0:T(8,128)}, f32[256,2048]{1,0:T(...) custom-call(bf16[2,128,2048]{2,1,0:T(8,128)(2,1)} %bitcast.6, ...), custom_call_target="tpu_custom_call" | custom-call | flops 51539607552 | bytes 103079216 | tf_op jit(solution)/shard_map/pallas_call | solution.py:440
  226.4 0.0 copy-start.2
  226.4 0.0 copy-start.3
  226.4 4.0 %add.9 = f32[2048,256]{1,0:T(8,128)} add(f32[2048,256]{1,0:T(8,128)} %get-tuple-element.12, f32[2048,256]{1,0:T(8,128)} %get-tuple-element.13) | non-fusion elementwise | flops 524288 | bytes 6291456 | tf_op jit(solution)/shard_map/add | solution.py:482
  230.4 0.0 copy-done.2
  230.4 0.0 copy-done.3
  230.4 0.0 copy-start
  230.4 0.0 copy-start.1
  230.4 1.6 add.10
  232.0 0.7 copy-done
  232.8 0.6 copy-done.1
  233.4 0.0 copy-start.4
  233.4 1.6 add.11
  235.0 0.0 copy-done.4
  235.0 1.0 copy.12
Async XLA Ops:
  226.4 4.0 %copy-start.2 = (f32[2048,256]{1,0:T(8,128)S(1)}, f32[2048,256]{1,0:T(8,128)}, u32[]{:S(2)}) copy-start(f32[2048,256]{1,0:T(8,128)} %get-tuple-element.14) | copy-start | bytes 6291460
  226.4 4.0 %copy-start.3 = (f32[2048,256]{1,0:T(8,128)S(1)}, f32[2048,256]{1,0:T(8,128)}, u32[]{:S(2)}) copy-start(f32[2048,256]{1,0:T(8,128)} %get-tuple-element.15) | copy-start | bytes 6291460
  230.4 2.3 copy-start
  230.4 3.0 %copy-start.1 = (f32[256,2048]{1,0:T(8,128)S(1)}, f32[256,2048]{1,0:T(8,128)}, u32[]{:S(2)}) copy-start(f32[256,2048]{1,0:T(8,128)} %get-tuple-element.17) | copy-start | bytes 6291460
  233.4 1.6 copy-start.4

commit v5 on v4

--- a/solution.py
+++ b/solution.py
@@ -12,12 +12,13 @@
 BF16 = jnp.bfloat16
 S = 4
 MESH = pl.DeviceIdType.MESH
+SPLIT = 3
 PLAN = (
-    "W0", "a0", "c0", "U0", "Y1", "L0", "a1", "O1", "c1", "U1", "A0", "C0", "U2", "Y2", "U3", "a2", "E2",
-    "c2", "A1", "C1", "Y3", "A2", "W1", "a3", "C2", "A3", "O3", "W2", "L1", "c3", "C3", "Y4", "a4", "Y5",
-    "U4", "P1", "a5", "P2", "U5", "R2", "R3", "P3", "U6", "E4", "Y6", "c4", "A4", "R4", "a6", "C4", "R5",
-    "P4", "U7", "A5", "A6", "O5", "L2", "c5", "C5", "Y7", "a7", "A7", "S0", "E6", "R6", "R7", "c6", "P5",
-    "C6", "O7", "c7", "C7", "S1", "R8", "R9", "P6", "R10", "R11", "P7", "R12", "R13", "P8", "R14", "R15",
+    "W1", "U2", "U0", "W0", "Y1", "a0", "a1", "L0", "Y2", "U1", "Y3", "W2", "A0", "c0", "E2", "a2", "C0",
+    "U3", "O1", "A1", "c1", "Y4", "A2", "P1", "R2", "P2", "a3", "L1", "U4", "Y5", "R3", "U5", "c2", "C1",
+    "A3", "a4", "C2", "E4", "O3", "c3", "Y6", "c4", "U6", "P3", "C3", "a5", "A4", "O5", "U7", "R4", "A5",
+    "C4", "a6", "L2", "R5", "Y7", "A6", "a7", "A7", "c5", "E6", "S0", "C5", "c6", "P4", "R6", "C6", "O7",
+    "c7", "R7", "C7", "R8", "S1", "P5", "R9", "R10", "P6", "R11", "R12", "P7", "R13", "R14", "P8", "R15",
 )
 KINDS = "YLEOacACPRSUW"
 
@@ -82,11 +83,21 @@
         src, land, ss, rs = rows[i][:4]
         return remote(src.at[d] if first else land.at[s, core, d], land.at[s + 1, core, d], ss.at[s, d], rs.at[s + 1, d], down[d])
 
-    def away(k, d, first=False):
-        return remote(x_h.at[d] if first else xl.at[2 * k, core, d], rl.at[k, d], b_s.at[k, d], b_r.at[k, d], leave[d])
-
-    def relay(k, d):
-        return remote(rl.at[k, d], xl.at[2 * k + 2, core, d], l_s.at[k, d], xr_r.at[2 * k + 2, d], leave[d])
+    last = side - 2
+    hz = SPLIT * hb // 4
+
+    def spill(d):
+        s, rws = m - 3, pl.ds(hz, hb - hz)
+        return remote(xl.at[s, core, d, rws], xl.at[s + 1, core, d, rws], xr_s.at[s, d], xr_r.at[0, d], down[d])
+
+    def away(k, d, first=False, part=False):
+        rws = pl.ds(0, hz if part else hb)
+        src = x_h.at[d] if first else xl.at[2 * k, core, d, rws]
+        return remote(src, rl.at[k, d, rws], b_s.at[k, d], b_r.at[k, d], leave[d])
+
+    def relay(k, d, part=False):
+        rws = pl.ds(0, hz if part else hb)
+        return remote(rl.at[k, d, rws], xl.at[2 * k + 2, core, d, rws], l_s.at[k, d], xr_r.at[2 * k + 2, d], leave[d])
 
     def cross(i, s, d, first=False):
         src, land, ss, rs = rows[i][0], rows[i][1], rows[i][4], rows[i][5]
@@ -201,25 +212,44 @@
             cross(0, s, d).start()
 
     def relay_x(k):
-        for d in range(2):
-            away(k, d).wait_recv()
-            relay(k, d).start()
+        for part in (False, True):
+            @pl.when((k == last) == part)
+            def _(part=part):
+                for d in range(2):
+                    away(k, d, part=part).wait_recv()
+                    relay(k, d, part).start()
 
     def pass_even_x(s):
         k = s // 2
         for d in range(2):
-            relay(k - 1, d).wait_recv()
-
-            @pl.when(s < m - 2)
+            @pl.when(k - 1 < last)
+            def _(d=d):
+                relay(k - 1, d).wait_recv()
+
+            @pl.when(k - 1 == last)
+            def _(d=d):
+                relay(k - 1, d, True).wait_recv()
+                spill(d).wait_recv()
+
+            @pl.when(k < last)
             def _(d=d):
                 away(k, d).start()
 
+            @pl.when(k == last)
+            def _(d=d):
+                away(k, d, part=True).start()
+
             ring(1, s, d).start()
             cross(1, s, d).start()
 
     def take_odd_x(s):
         for d in range(2):
             ring(1, s - 1, d).wait_recv()
+
+            @pl.when(s == m - 3)
+            def _(d=d):
+                spill(d).start()
+
             cross(1, s, d).start()
 
     def grads(t):
@@ -414,10 +444,19 @@
     lax.fori_loop(0, m, drain, 0)
     for k in range(side - 1):
         for d in range(2):
-            away(k, d).wait_send()
-            relay(k, d).wait_send()
+            away(k, d, part=k == last).wait_send()
+            relay(k, d, k == last).wait_send()
+    for d in range(2):
+        spill(d).wait_send()
     for c in outs:
         c.wait()
+
+
+def finish(dx, own_d, own_g, own_u, rec_d, rec_g, rec_u, dx_o, d_o, g_o, u_o):
+    dx_o[...] = dx[...]
+    d_o[...] = own_d[...] + rec_d[...]
+    g_o[...] = own_g[...] + rec_g[...]
+    u_o[...] = own_u[...] + rec_u[...]
 
 
 def solution(mesh):
@@ -479,7 +518,19 @@
             x.reshape(2, hb, h), dy.reshape(2, hb, h), wg, wu, wd,
             ug.reshape(n, 2, 2, hb, fb), uu.reshape(n, 2, 2, hb, fb),
         )
-        return dx, own_g + rec_g, own_u + rec_u, own_d + rec_d
+        grid = 4
+
+        def spec(r, c):
+            return pl.BlockSpec((r // grid, c), lambda i: (i, 0))
+
+        dx, dwd, dwg, dwu = pl.pallas_call(
+            finish,
+            grid=(grid,),
+            out_shape=(sds((tb, h), BF16), sds((fb, h), F32), sds((h, fb), F32), sds((h, fb), F32)),
+            in_specs=[spec(tb, h)] + [spec(fb, h), spec(h, fb), spec(h, fb)] * 2,
+            out_specs=[spec(tb, h), spec(fb, h), spec(h, fb), spec(h, fb)],
+        )(dx, own_d, own_g, own_u, rec_d, rec_g, rec_u)
+        return dx, dwg, dwu, dwd
 
     return jax.shard_map(
         body, mesh=mesh, in_specs=(tok, tok, col, col, row, act, act), out_specs=(tok, act, act, tok), check_vma=False

time: 236 us -> 229 us (0.970)
  other arithmetic: 7.14 us -> 0 us
  local copies, waits for them, and re-layouts: 2.36 us -> 0 us
    pallas_call x0 -> x1, Pallas kernels: none -> 7.84 us  [body(): pl.pallas_call(finish, grid=(grid,), out_shape=(sds((tb, h), BF16), sds((...]
    add x3 -> x0, other arithmetic: 7.14 us -> none  [body(): return (dx, own_g + rec_g, own_u + rec_u, own_d + rec_d)]
    pallas_call x1, Pallas kernels: 226 us -> 221 us  [body(): pl.pallas_call(functools.partial(kernel, side), out_shape=(sds((tb, h), B...]
    unnamed x11 -> x0, local copies, waits for them, and re-layouts: 2.36 us -> none
where the time goes in v5:
time: 229 us
  Pallas kernels  228 us (100%)
    pallas_call x1, Pallas kernels, body(): pl.pallas_call(functools.partial(kernel, side), out_shape=(sds((tb, h), B...  221 us
    pallas_call x1, Pallas kernels, body(): pl.pallas_call(finish, grid=(grid,), out_shape=(sds((tb, h), BF16), sds((...  7.84 us

profile of v5, /device:TPU:97, one launch (start us, length us, event | category | flops | bytes accessed | tf_op | source)
XLA Modules:
  0.0 229.0 jit_solution(8057369907880700796)
XLA Ops:
  0.6 220.6 %shard_map.102 = (bf16[256,2048]{1,0:T(8,128)(2,1)}, f32[256,2048]{1,0:T(8,128)}, f32[2048,256]{1,0:T(8,128)}, f32[2048,256]{1,0:T(8,128)}, f32[256,2048]{1,0:T(...) custom-call(bf16[2,128,2048]{2,1,0:T(8,128)(2,1)} %bitcast.6, ...), custom_call_target="tpu_custom_call" | custom-call | flops 51539607552 | bytes 103079216 | tf_op jit(solution)/shard_map/pallas_call | solution.py:479
  221.2 7.8 %shard_map.103 = (bf16[256,2048]{1,0:T(8,128)(2,1)}, f32[256,2048]{1,0:T(8,128)}, f32[2048,256]{1,0:T(8,128)}, f32[2048,256]{1,0:T(8,128)}) custom-call(bf16[256,2048]{1,0:T(8,128)(2,1)} %get-tuple-element.15.dx, f32[256,2048]{1,0:T(8,128)} %get-tuple-element.16.own_d, f32[2048,256]{1,0:T(8,128)} %get-tuple-element.17.own_g, ...), custom_call_target="tpu_custom_call" | custom-call | tf_op jit(solution)/shard_map/pallas_call | solution.py:526

commit v6 on v5

--- a/solution.py
+++ b/solution.py
@@ -12,15 +12,16 @@
 BF16 = jnp.bfloat16
 S = 4
 MESH = pl.DeviceIdType.MESH
-SPLIT = 3
+SPLIT = 6
 PLAN = (
     "W1", "U2", "U0", "W0", "Y1", "a0", "a1", "L0", "Y2", "U1", "Y3", "W2", "A0", "c0", "E2", "a2", "C0",
     "U3", "O1", "A1", "c1", "Y4", "A2", "P1", "R2", "P2", "a3", "L1", "U4", "Y5", "R3", "U5", "c2", "C1",
     "A3", "a4", "C2", "E4", "O3", "c3", "Y6", "c4", "U6", "P3", "C3", "a5", "A4", "O5", "U7", "R4", "A5",
     "C4", "a6", "L2", "R5", "Y7", "A6", "a7", "A7", "c5", "E6", "S0", "C5", "c6", "P4", "R6", "C6", "O7",
-    "c7", "R7", "C7", "R8", "S1", "P5", "R9", "R10", "P6", "R11", "R12", "P7", "R13", "R14", "P8", "R15",
+    "c7", "R7", "C7", "R8", "S1", "P5", "R9", "R10", "P6", "R11", "R12", "P7", "R13", "R14", "P8", "D0", "D1",
+    "R15",
 )
-KINDS = "YLEOacACPRSUW"
+KINDS = "YLEOacACPRSDUW"
 
 
 def dot(a, b, ca, cb):
@@ -30,8 +31,8 @@
 def kernel(
     side,
     x_h, dy_h, wg_h, wu_h, wd_h, ug_h, uu_h,
-    dx_h, own_d, own_g, own_u, rec_d, rec_g, rec_u, dyl, xl, rl,
-    dyt, xt, uo, ux, wdb, wgu, gbuf, zb, dub, accd, accw, pbuf, sin, sout, rsb, rso,
+    dx_h, dwd_h, dwg_h, own_u, rec_u, dyl, xl, rl,
+    dyt, xt, uo, ux, wdb, wgu, gbuf, zb, dub, accd, accw, pbuf, sin, sout, rsb, rso, rec_d, rec_g,
     dyr_s, dyr_r, dyc_s, dyc_r, xr_s, xr_r, xc_s, xc_r, dyt_l, xt_l, u_s, u_r, u_l,
     w_s, w_r, w_l, p_s, p_r, rs_s, rs_r, e_s, e_r, o_l, b_s, b_r, l_s,
 ):
@@ -84,7 +85,7 @@
         return remote(src.at[d] if first else land.at[s, core, d], land.at[s + 1, core, d], ss.at[s, d], rs.at[s + 1, d], down[d])
 
     last = side - 2
-    hz = SPLIT * hb // 4
+    hz = SPLIT * hb // 8
 
     def spill(d):
         s, rws = m - 3, pl.ds(hz, hb - hz)
@@ -166,8 +167,8 @@
 
     def own_out(i):
         if i == 0:
-            return pltpu.make_async_copy(accd.at[pl.ds(0, fb)], own_d, o_l.at[0])
-        return pltpu.make_async_copy(accw.at[:, pl.ds((i - 1) * 2 * fb, fb)], (own_g, own_u)[i - 1], o_l.at[i])
+            return pltpu.make_async_copy(accd.at[pl.ds(0, fb)], dwd_h, o_l.at[0])
+        return pltpu.make_async_copy(accw.at[:, pl.ds((i - 1) * 2 * fb, fb)], (dwg_h, own_u)[i - 1], o_l.at[i])
 
     def rs_hop(j, d, z):
         a, b = lax.rem(j, 2), lax.rem(j + 1, S)
@@ -378,7 +379,23 @@
                 for w in which:
                     for k in range(2):
                         swap(w, k).start()
-                    own_out(w).start()
+                    if w == 2:
+                        own_out(w).start()
+
+    def fold(i):
+        @pl.when(i == 0)
+        def _():
+            for k in range(2):
+                swap(0, k).wait_recv()
+            accd[0:fb, :] += rec_d[...]
+            own_out(0).start()
+
+        @pl.when(i == 1)
+        def _():
+            for k in range(2):
+                swap(1, k).wait_recv()
+            accw[:, 0:fb] += rec_g[...]
+            own_out(1).start()
 
     def send_weight(i):
         for w in range(3):
@@ -389,7 +406,7 @@
 
     work = dict(
         Y=pass_dy, L=relay_x, E=pass_even_x, O=take_odd_x, a=lambda t: tile_load(0, t), c=lambda t: tile_load(1, t),
-        A=grads, C=weight_grads, P=partial, R=pass_sum, S=swaps, U=u_send, W=send_weight,
+        A=grads, C=weight_grads, P=partial, R=pass_sum, S=swaps, D=fold, U=u_send, W=send_weight,
     )
     packed = [KINDS.index(w[0]) * 16 + int(w[1:]) for w in PLAN]
 
@@ -421,7 +438,9 @@
     for i in range(3):
         own_out(i).wait()
         for k in range(2):
-            swap(i, k).wait()
+            swap(i, k).wait_send()
+            if i == 2:
+                swap(i, k).wait_recv()
             w_remote(i, k).wait_send()
     for j in (m - 1, m):
         part_hop(j).wait_send()
@@ -452,10 +471,10 @@
         c.wait()
 
 
-def finish(dx, own_d, own_g, own_u, rec_d, rec_g, rec_u, dx_o, d_o, g_o, u_o):
+def finish(dx, dwd, dwg, own_u, rec_u, dx_o, d_o, g_o, u_o):
     dx_o[...] = dx[...]
-    d_o[...] = own_d[...] + rec_d[...]
-    g_o[...] = own_g[...] + rec_g[...]
+    d_o[...] = dwd[...]
+    g_o[...] = dwg[...]
     u_o[...] = own_u[...] + rec_u[...]
 
 
@@ -476,16 +495,15 @@
         dma = pltpu.SemaphoreType.DMA
         sds = jax.ShapeDtypeStruct
         flops = 12 * n * tb * h * 2 * fb
-        dx, own_d, own_g, own_u, rec_d, rec_g, rec_u, _, _, _ = pl.pallas_call(
+        dx, dwd, dwg, own_u, rec_u, _, _, _ = pl.pallas_call(
             functools.partial(kernel, side),
             out_shape=(
                 sds((tb, h), BF16),
-                sds((fb, h), F32), sds((h, fb), F32), sds((h, fb), F32),
-                sds((fb, h), F32), sds((h, fb), F32), sds((h, fb), F32),
+                sds((fb, h), F32), sds((h, fb), F32), sds((h, fb), F32), sds((h, fb), F32),
                 sds((m, 2, 2, hb, h), BF16), sds((m, 2, 2, hb, h), BF16), sds((side - 1, 2, hb, h), BF16),
             ),
             in_specs=[pl.BlockSpec(memory_space=pltpu.HBM)] * 7,
-            out_specs=[pl.BlockSpec(memory_space=pl.ANY)] * 10,
+            out_specs=[pl.BlockSpec(memory_space=pl.ANY)] * 8,
             scratch_shapes=[
                 vm((2, 2, 2, hb, h), BF16),
                 vm((2, 2, 2, hb, h), BF16),
@@ -503,6 +521,8 @@
                 vm((2, tb, h), BF16),
                 vm((S, 2, 2, hb // 2, h), BF16),
                 vm((2, 2, 2, hb // 2, h), BF16),
+                vm((fb, h), F32),
+                vm((h, fb), F32),
                 dma((m, 2)), dma((m, 2)), dma((m, 2)), dma((m, 2)),
                 dma((m, 2)), dma((m, 2)), dma((m, 2)), dma((m, 2)),
                 dma((2,)), dma((2,)), dma((m, 2)), dma((m, 2)), dma((2,)),
@@ -527,9 +547,9 @@
             finish,
             grid=(grid,),
             out_shape=(sds((tb, h), BF16), sds((fb, h), F32), sds((h, fb), F32), sds((h, fb), F32)),
-            in_specs=[spec(tb, h)] + [spec(fb, h), spec(h, fb), spec(h, fb)] * 2,
+            in_specs=[spec(tb, h), spec(fb, h)] + [spec(h, fb)] * 3,
             out_specs=[spec(tb, h), spec(fb, h), spec(h, fb), spec(h, fb)],
-        )(dx, own_d, own_g, own_u, rec_d, rec_g, rec_u)
+        )(dx, dwd, dwg, own_u, rec_u)
         return dx, dwg, dwu, dwd
 
     return jax.shard_map(

time: 229 us -> 228 us (level)
  no operation moved by 1% of the time
where the time goes in v6:
time: 228 us
  Pallas kernels  227 us (100%)
    pallas_call x1, Pallas kernels, body(): pl.pallas_call(functools.partial(kernel, side), out_shape=(sds((tb, h), B...  221 us
    pallas_call x1, Pallas kernels, body(): pl.pallas_call(finish, grid=(grid,), out_shape=(sds((tb, h), BF16), sds((...  6.83 us

profile of v6, /device:TPU:97, one launch (start us, length us, event | category | flops | bytes accessed | tf_op | source)
XLA Modules:
  0.0 228.0 jit_solution(10882643098534475912)
XLA Ops:
  0.6 220.5 %shard_map.102 = (bf16[256,2048]{1,0:T(8,128)(2,1)}, f32[256,2048]{1,0:T(8,128)}, f32[2048,256]{1,0:T(8,128)}, f32[2048,256]{1,0:T(8,128)}, f32[2048,256]{1,0:T(...) custom-call(bf16[2,128,2048]{2,1,0:T(8,128)(2,1)} %bitcast.6, ...), custom_call_target="tpu_custom_call" | custom-call | flops 51539607552 | bytes 103079216 | tf_op jit(solution)/shard_map/pallas_call | solution.py:498
  221.2 6.8 %shard_map.103 = (bf16[256,2048]{1,0:T(8,128)(2,1)}, f32[256,2048]{1,0:T(8,128)}, f32[2048,256]{1,0:T(8,128)}, f32[2048,256]{1,0:T(8,128)}) custom-call(bf16[256,2048]{1,0:T(8,128)(2,1)} %get-tuple-element.13.dx, f32[256,2048]{1,0:T(8,128)} %get-tuple-element.14.dwd, f32[2048,256]{1,0:T(8,128)} %get-tuple-element.15.dwg, ...), custom_call_target="tpu_custom_call" | custom-call | tf_op jit(solution)/shard_map/pallas_call | solution.py:546

commit v7 on v6

--- a/solution.py
+++ b/solution.py
@@ -12,13 +12,13 @@
 BF16 = jnp.bfloat16
 S = 4
 MESH = pl.DeviceIdType.MESH
-SPLIT = 6
+SPLIT = (6, 6, 8)
 PLAN = (
-    "W1", "U2", "U0", "W0", "Y1", "a0", "a1", "L0", "Y2", "U1", "Y3", "W2", "A0", "c0", "E2", "a2", "C0",
-    "U3", "O1", "A1", "c1", "Y4", "A2", "P1", "R2", "P2", "a3", "L1", "U4", "Y5", "R3", "U5", "c2", "C1",
-    "A3", "a4", "C2", "E4", "O3", "c3", "Y6", "c4", "U6", "P3", "C3", "a5", "A4", "O5", "U7", "R4", "A5",
-    "C4", "a6", "L2", "R5", "Y7", "A6", "a7", "A7", "c5", "E6", "S0", "C5", "c6", "P4", "R6", "C6", "O7",
-    "c7", "R7", "C7", "R8", "S1", "P5", "R9", "R10", "P6", "R11", "R12", "P7", "R13", "R14", "P8", "D0", "D1",
+    "U0", "a0", "W0", "W2", "c0", "Y1", "L0", "A0", "U1", "O1", "a1", "Y2", "c1", "W1", "U2", "C0", "E2",
+    "U3", "a2", "Y3", "A1", "O3", "c2", "P1", "Y4", "A2", "L1", "U4", "R2", "U5", "C1", "C2", "R3", "a3",
+    "Y5", "a4", "c3", "E4", "A3", "C3", "c4", "A4", "U6", "P2", "Y6", "P3", "a5", "R4", "L2", "A5", "C4",
+    "U7", "a6", "A6", "Y7", "E6", "O5", "a7", "R5", "c5", "A7", "S0", "P4", "C5", "c6", "O7", "R6", "c7",
+    "C6", "R7", "C7", "R8", "S1", "P5", "D0", "R9", "R10", "P6", "R11", "R12", "P7", "R13", "R14", "D1", "P8",
     "R15",
 )
 KINDS = "YLEOacACPRSDUW"
@@ -34,7 +34,7 @@
     dx_h, dwd_h, dwg_h, own_u, rec_u, dyl, xl, rl,
     dyt, xt, uo, ux, wdb, wgu, gbuf, zb, dub, accd, accw, pbuf, sin, sout, rsb, rso, rec_d, rec_g,
     dyr_s, dyr_r, dyc_s, dyc_r, xr_s, xr_r, xc_s, xc_r, dyt_l, xt_l, u_s, u_r, u_l,
-    w_s, w_r, w_l, p_s, p_r, rs_s, rs_r, e_s, e_r, o_l, b_s, b_r, l_s,
+    w_s, w_r, w_l, p_s, p_r, rs_s, rs_r, e_s, e_r, o_l, b_s, b_r, l_s, z_r,
 ):
     _, hb, h = dy_h.shape
     tb = 2 * hb
@@ -84,20 +84,19 @@
         src, land, ss, rs = rows[i][:4]
         return remote(src.at[d] if first else land.at[s, core, d], land.at[s + 1, core, d], ss.at[s, d], rs.at[s + 1, d], down[d])
 
-    last = side - 2
-    hz = SPLIT * hb // 8
-
-    def spill(d):
-        s, rws = m - 3, pl.ds(hz, hb - hz)
-        return remote(xl.at[s, core, d, rws], xl.at[s + 1, core, d, rws], xr_s.at[s, d], xr_r.at[0, d], down[d])
-
-    def away(k, d, first=False, part=False):
-        rws = pl.ds(0, hz if part else hb)
-        src = x_h.at[d] if first else xl.at[2 * k, core, d, rws]
+    near = [e * hb // 8 for e in SPLIT]
+
+    def spill(k, d):
+        s, rws = 2 * k + 1, pl.ds(near[k], hb - near[k])
+        return remote(xl.at[s, core, d, rws], xl.at[s + 1, core, d, rws], xr_s.at[s, d], z_r.at[k, d], down[d])
+
+    def away(k, d, first=False):
+        rws = pl.ds(0, near[k])
+        src = x_h.at[d, rws] if first else xl.at[2 * k, core, d, rws]
         return remote(src, rl.at[k, d, rws], b_s.at[k, d], b_r.at[k, d], leave[d])
 
-    def relay(k, d, part=False):
-        rws = pl.ds(0, hz if part else hb)
+    def relay(k, d):
+        rws = pl.ds(0, near[k])
         return remote(rl.at[k, d, rws], xl.at[2 * k + 2, core, d, rws], l_s.at[k, d], xr_r.at[2 * k + 2, d], leave[d])
 
     def cross(i, s, d, first=False):
@@ -212,34 +211,29 @@
 
             cross(0, s, d).start()
 
+    def each_piece(k, do):
+        for kk in range(side - 1):
+            @pl.when(k == kk)
+            def _(kk=kk):
+                for d in range(2):
+                    do(kk, d)
+
     def relay_x(k):
-        for part in (False, True):
-            @pl.when((k == last) == part)
-            def _(part=part):
-                for d in range(2):
-                    away(k, d, part=part).wait_recv()
-                    relay(k, d, part).start()
+        def do(kk, d):
+            away(kk, d).wait_recv()
+            relay(kk, d).start()
+
+        each_piece(k, do)
 
     def pass_even_x(s):
-        k = s // 2
-        for d in range(2):
-            @pl.when(k - 1 < last)
-            def _(d=d):
-                relay(k - 1, d).wait_recv()
-
-            @pl.when(k - 1 == last)
-            def _(d=d):
-                relay(k - 1, d, True).wait_recv()
-                spill(d).wait_recv()
-
-            @pl.when(k < last)
-            def _(d=d):
-                away(k, d).start()
-
-            @pl.when(k == last)
-            def _(d=d):
-                away(k, d, part=True).start()
-
+        def arrived(kk, d):
+            relay(kk, d).wait_recv()
+            if near[kk] < hb:
+                spill(kk, d).wait_recv()
+
+        each_piece(s // 2 - 1, arrived)
+        each_piece(s // 2, lambda kk, d: away(kk, d).start())
+        for d in range(2):
             ring(1, s, d).start()
             cross(1, s, d).start()
 
@@ -247,10 +241,12 @@
         for d in range(2):
             ring(1, s - 1, d).wait_recv()
 
-            @pl.when(s == m - 3)
-            def _(d=d):
-                spill(d).start()
-
+        def pass_rest(kk, d):
+            if near[kk] < hb:
+                spill(kk, d).start()
+
+        each_piece(s // 2, pass_rest)
+        for d in range(2):
             cross(1, s, d).start()
 
     def grads(t):
@@ -463,10 +459,10 @@
     lax.fori_loop(0, m, drain, 0)
     for k in range(side - 1):
         for d in range(2):
-            away(k, d, part=k == last).wait_send()
-            relay(k, d, k == last).wait_send()
-    for d in range(2):
-        spill(d).wait_send()
+            away(k, d).wait_send()
+            relay(k, d).wait_send()
+            if near[k] < hb:
+                spill(k, d).wait_send()
     for c in outs:
         c.wait()
 
@@ -528,7 +524,7 @@
                 dma((2,)), dma((2,)), dma((m, 2)), dma((m, 2)), dma((2,)),
                 dma((3, 2)), dma((3, 2)), dma((3,)), dma((2,)), dma((S,)),
                 dma((2, 2, 2)), dma((S, 2, 2)), dma((3, 2)), dma((3, 2)), dma((7,)),
-                dma((side - 1, 2)), dma((side - 1, 2)), dma((side - 1, 2)),
+                dma((side - 1, 2)), dma((side - 1, 2)), dma((side - 1, 2)), dma((side - 1, 2)),
             ],
             compiler_params=pltpu.CompilerParams(
                 collective_id=0, has_side_effects=True, vmem_limit_bytes=62 * 1024 * 1024

time: 228 us -> 227 us (level)
  no operation moved by 1% of the time
where the time goes in v7:
time: 227 us
  Pallas kernels  226 us (100%)
    pallas_call x1, Pallas kernels, body(): pl.pallas_call(functools.partial(kernel, side), out_shape=(sds((tb, h), B...  220 us
    pallas_call x1, Pallas kernels, body(): pl.pallas_call(finish, grid=(grid,), out_shape=(sds((tb, h), BF16), sds((...  6.83 us

profile of v7, /device:TPU:97, one launch (start us, length us, event | category | flops | bytes accessed | tf_op | source)
XLA Modules:
  0.0 227.0 jit_solution(478792783692949230)
XLA Ops:
  0.6 219.5 %shard_map.102 = (bf16[256,2048]{1,0:T(8,128)(2,1)}, f32[256,2048]{1,0:T(8,128)}, f32[2048,256]{1,0:T(8,128)}, f32[2048,256]{1,0:T(8,128)}, f32[2048,256]{1,0:T(...) custom-call(bf16[2,128,2048]{2,1,0:T(8,128)(2,1)} %bitcast.6, ...), custom_call_target="tpu_custom_call" | custom-call | flops 51539607552 | bytes 103079216 | tf_op jit(solution)/shard_map/pallas_call | solution.py:494
  220.2 6.8 %shard_map.103 = (bf16[256,2048]{1,0:T(8,128)(2,1)}, f32[256,2048]{1,0:T(8,128)}, f32[2048,256]{1,0:T(8,128)}, f32[2048,256]{1,0:T(8,128)}) custom-call(bf16[256,2048]{1,0:T(8,128)(2,1)} %get-tuple-element.13.dx, f32[256,2048]{1,0:T(8,128)} %get-tuple-element.14.dwd, f32[2048,256]{1,0:T(8,128)} %get-tuple-element.15.dwg, ...), custom_call_target="tpu_custom_call" | custom-call | tf_op jit(solution)/shard_map/pallas_call | solution.py:542

commit v8 on v7

--- a/solution.py
+++ b/solution.py
@@ -12,13 +12,13 @@
 BF16 = jnp.bfloat16
 S = 4
 MESH = pl.DeviceIdType.MESH
-SPLIT = (6, 6, 8)
+SPLIT = (7, 6, 8)
 PLAN = (
-    "U0", "a0", "W0", "W2", "c0", "Y1", "L0", "A0", "U1", "O1", "a1", "Y2", "c1", "W1", "U2", "C0", "E2",
-    "U3", "a2", "Y3", "A1", "O3", "c2", "P1", "Y4", "A2", "L1", "U4", "R2", "U5", "C1", "C2", "R3", "a3",
-    "Y5", "a4", "c3", "E4", "A3", "C3", "c4", "A4", "U6", "P2", "Y6", "P3", "a5", "R4", "L2", "A5", "C4",
-    "U7", "a6", "A6", "Y7", "E6", "O5", "a7", "R5", "c5", "A7", "S0", "P4", "C5", "c6", "O7", "R6", "c7",
-    "C6", "R7", "C7", "R8", "S1", "P5", "D0", "R9", "R10", "P6", "R11", "R12", "P7", "R13", "R14", "D1", "P8",
+    "U1", "U0", "c0", "W0", "L0", "Y1", "a0", "O1", "Y2", "W2", "W1", "a1", "E2", "A0", "a2", "C0", "Y3",
+    "c1", "U2", "U4", "A1", "U3", "O3", "U5", "C1", "P1", "Y4", "R2", "A2", "a3", "Y5", "c2", "P2", "L1",
+    "R3", "U6", "A3", "P3", "a4", "Y6", "E4", "C2", "R4", "a5", "c3", "c4", "A4", "U7", "A5", "a6", "Y7",
+    "L2", "R5", "C3", "A6", "a7", "P4", "O5", "A7", "E6", "c5", "S0", "C4", "R6", "R7", "c6", "C5", "C6",
+    "O7", "c7", "C7", "R8", "S1", "R9", "P5", "P6", "R10", "R11", "R12", "P7", "D0", "D1", "R13", "R14", "P8",
     "R15",
 )
 KINDS = "YLEOacACPRSDUW"

time: 227 us -> 226 us (level)
  no operation moved by 1% of the time
where the time goes in v8:
time: 226 us
  Pallas kernels  225 us (100%)
    pallas_call x1, Pallas kernels, body(): pl.pallas_call(functools.partial(kernel, side), out_shape=(sds((tb, h), B...  218 us
    pallas_call x1, Pallas kernels, body(): pl.pallas_call(finish, grid=(grid,), out_shape=(sds((tb, h), BF16), sds((...  6.83 us

profile of v8, /device:TPU:97, one launch (start us, length us, event | category | flops | bytes accessed | tf_op | source)
XLA Modules:
  0.0 225.7 jit_solution(6817930530133213807)
XLA Ops:
  0.6 218.2 %shard_map.102 = (bf16[256,2048]{1,0:T(8,128)(2,1)}, f32[256,2048]{1,0:T(8,128)}, f32[2048,256]{1,0:T(8,128)}, f32[2048,256]{1,0:T(8,128)}, f32[2048,256]{1,0:T(...) custom-call(bf16[2,128,2048]{2,1,0:T(8,128)(2,1)} %bitcast.6, ...), custom_call_target="tpu_custom_call" | custom-call | flops 51539607552 | bytes 103079216 | tf_op jit(solution)/shard_map/pallas_call | solution.py:494
  218.9 6.8 %shard_map.103 = (bf16[256,2048]{1,0:T(8,128)(2,1)}, f32[256,2048]{1,0:T(8,128)}, f32[2048,256]{1,0:T(8,128)}, f32[2048,256]{1,0:T(8,128)}) custom-call(bf16[256,2048]{1,0:T(8,128)(2,1)} %get-tuple-element.13.dx, f32[256,2048]{1,0:T(8,128)} %get-tuple-element.14.dwd, f32[2048,256]{1,0:T(8,128)} %get-tuple-element.15.dwg, ...), custom_call_target="tpu_custom_call" | custom-call | tf_op jit(solution)/shard_map/pallas_call | solution.py:542
